TPU v7x, 32 devices: a 4x4x1 block of a 4x4x8 slice. The times are simulated.
32 devices in a mesh: dp: 1 (over z), tp: 4 (over y), ep: 8 (over x, core).
Axes of the slice: x: 4, y: 4, z: 1, core: 2. Of those that a mesh axis runs over, the one named last changes fastest.
The devices are a block of a 4x4x8 slice.
Arguments:
- hidden_in: bfloat16 [1024, 2048], P(('dp', 'ep'))
- topk_idx: int32 [1024, 6], P(('dp', 'ep'))
- norm_gain: bfloat16 [2048], replicated
- router_w: bfloat16 [2048, 64], replicated
- shared_sig_w: bfloat16 [2048, 1], replicated
- exp_gate: bfloat16 [64, 2048, 1408], P('ep', None, 'tp')
- exp_up: bfloat16 [64, 2048, 1408], P('ep', None, 'tp')
- exp_down: bfloat16 [64, 1408, 2048], P('ep', 'tp')
- sh_gate: bfloat16 [2048, 2816], P(None, ('tp', 'ep'))
- sh_up: bfloat16 [2048, 2816], P(None, ('tp', 'ep'))
- sh_down: bfloat16 [2816, 2048], P(('tp', 'ep'))
Outputs:
- output: bfloat16 [1024, 2048], P(('dp', 'ep'))
All inputs are finite; a program needn't handle non-finite values.
Results may differ from a plain program's by a relative error of at most 0.0123824.
Values are sent between devices in bfloat16 or wider.
A program may use at most 768 MiB of HBM per device.

v0:
```python
import jax
import jax.numpy as jnp
from jax import lax
from jax.sharding import PartitionSpec as P

RMS_EPS = 1e-6


def rms_norm(rows, gain):
    rows_f32 = rows.astype(jnp.float32)
    inv_rms = lax.rsqrt(jnp.mean(rows_f32 * rows_f32, axis=-1, keepdims=True) + RMS_EPS)
    return (rows_f32 * inv_rms * gain.astype(jnp.float32)).astype(jnp.bfloat16)


def routed_part(all_h, all_idx, all_wt, exp_gate, exp_up, exp_down, ep_rank):
    n_tok, n_top = all_idx.shape
    n_local = exp_gate.shape[0]
    n_rows = n_tok * min(n_top, n_local)
    local_id = all_idx.reshape(-1) - ep_rank * n_local
    is_local = (local_id >= 0) & (local_id < n_local)
    sort_key = jnp.where(is_local, local_id, n_local)
    order = jnp.argsort(sort_key, stable=True)[:n_rows]
    tok_ids = order // n_top
    row_wts = jnp.where(is_local, all_wt.reshape(-1), 0.0)[order]
    counts = jax.ops.segment_sum(jnp.ones_like(sort_key), sort_key, num_segments=n_local + 1)[:n_local]
    rows = jnp.take(all_h, tok_ids, axis=0)
    gate_val = lax.ragged_dot(rows, exp_gate, counts, preferred_element_type=jnp.float32)
    up_val = lax.ragged_dot(rows, exp_up, counts, preferred_element_type=jnp.float32)
    act_val = (jax.nn.silu(gate_val) * up_val).astype(jnp.bfloat16)
    down_val = lax.ragged_dot(act_val, exp_down, counts, preferred_element_type=jnp.float32)
    return jax.ops.segment_sum(down_val * row_wts[:, None], tok_ids, num_segments=n_tok)


def solution(mesh):
    tok_spec = P(('dp', 'ep'), None)
    in_specs = (tok_spec, tok_spec, P(None), P(None, None), P(None, None),
                P('ep', None, 'tp'), P('ep', None, 'tp'), P('ep', 'tp', None),
                P(None, ('tp', 'ep')), P(None, ('tp', 'ep')), P(('tp', 'ep'), None))

    def local_step(hidden_in, topk_idx, norm_gain, router_w, shared_sig_w, exp_gate, exp_up, exp_down, sh_gate, sh_up, sh_down):
        normed = rms_norm(hidden_in, norm_gain)
        router_prob = jax.nn.softmax(jnp.dot(normed, router_w, preferred_element_type=jnp.float32), axis=-1)
        chosen_wt = jnp.take_along_axis(router_prob, topk_idx, axis=1)
        sig_gate = jax.nn.sigmoid(jnp.dot(normed, shared_sig_w, preferred_element_type=jnp.float32))
        all_h = lax.all_gather(normed, 'ep', axis=0, tiled=True)
        all_idx = lax.all_gather(topk_idx, 'ep', axis=0, tiled=True)
        all_wt = lax.all_gather(chosen_wt, 'ep', axis=0, tiled=True)
        all_sig = lax.all_gather(sig_gate, 'ep', axis=0, tiled=True)
        routed = routed_part(all_h, all_idx, all_wt, exp_gate, exp_up, exp_down, lax.axis_index('ep'))
        sh_act = (jax.nn.silu(jnp.dot(all_h, sh_gate, preferred_element_type=jnp.float32)) * jnp.dot(all_h, sh_up, preferred_element_type=jnp.float32)).astype(jnp.bfloat16)
        shared = all_sig * jnp.dot(sh_act, sh_down, preferred_element_type=jnp.float32)
        partial_sum = (routed + shared).astype(jnp.bfloat16)
        own_rows = lax.psum_scatter(partial_sum, 'ep', scatter_dimension=0, tiled=True)
        total = lax.psum(own_rows, 'tp')
        return (hidden_in.astype(jnp.float32) + total.astype(jnp.float32)).astype(jnp.bfloat16)

    return jax.shard_map(local_step, mesh=mesh, in_specs=in_specs, out_specs=tok_spec, check_vma=False)
```

profile of v0, /device:TPU:97, one launch (start us, length us, event | category | flops | bytes accessed | tf_op | source)
XLA Modules:
  0.0 523.6 jit_solution(6006342830391733699)
XLA Ops:
  6.5 0.0 copy-start
  6.6 0.0 all-gather.4.cloned.1.call-start
  6.6 0.7 convert_element_type.26
  7.3 1.2 fusion.9
  8.5 2.0 fusion.11
  10.6 0.1 all-gather.4.cloned.1.call-update
  10.6 0.1 reduce-scatter.2.cloned.1.call-start
  10.7 19.9 %all_gather.14 = s32[1024,6]{0,1:T(8,128)S(1)} all-gather(s32[128,6]{0,1:T(8,128)} %param.12), channel_id=1, replica_groups=mesh['dp'=1,'tp'=4,'ep'=8] {'ep'}, dimensions={0}, use_global_device_ids=true | all-gather | bytes 27648 | tf_op jit(solution)/shard_map/all_gather | solution.py:46
  30.6 0.2 copy.32
  30.8 0.3 sub.35
  31.2 0.4 sub.37
  31.6 43.5 %scatter_custom_fusion = s32[9]{0:T(128)} fusion(s32[6144]{0:T(1024)S(1)} %bitcast.30, s32[6144]{0:T(1024)S(1)} %ne.14, s32[]{:T(128)} %constant.34.clone.1), kind=kCustom, calls=%fused_computation.53 | custom fusion | flops 6144 | bytes 40 | tf_op jit(solution)/shard_map/scatter-add | solution.py:25
  75.1 1.6 ragged-dot-metadata
  76.7 16.2 %copy.35 = bf16[8,2048,352]{2,1,0:T(8,128)(2,1)} copy(bf16[8,2048,352]{1,2,0:T(8,128)(2,1)} %param.17) | data formatting | bytes 23068672 | tf_op args[6]
  92.9 0.0 copy-start.6
  92.9 0.0 copy-start.1
  92.9 0.0 copy-start.5
  92.9 15.4 %copy.34 = bf16[8,2048,352]{2,1,0:T(8,128)(2,1)} copy(bf16[8,2048,352]{1,2,0:T(8,128)(2,1)} %param.16) | data formatting | bytes 23068672 | tf_op args[5]
  108.3 0.0 copy-done.6
  108.3 0.1 copy.36
  108.4 0.1 reshape.83
  108.5 0.0 copy-done.1
  108.6 0.0 copy-done.5
  108.6 0.3 fusion.29
  108.9 5.1 gather_fusion.2
  114.1 0.1 reshape.86
  114.2 0.1 copy.37
  114.3 20.7 %all_gather.15 = f32[1024,6]{0,1:T(8,128)S(1)} all-gather(f32[128,6]{0,1:T(8,128)S(1)} %and_select_fusion.1), channel_id=1, replica_groups=mesh['dp'=1,'tp'=4,'ep'=8] {'ep'}, dimensions={0}, use_global_device_ids=true | all-gather | bytes 27648 | tf_op jit(solution)/shard_map/all_gather | solution.py:47
  135.0 0.2 copy.38
  135.2 0.3 reshape.66
  135.6 6.7 %sort.17 = (s32[6144]{0:T(1024)}, s32[6144]{0:T(1024)S(1)}) sort(s32[6144]{0:T(1024)S(1)} %fusion.25, s32[6144]{0:T(1024)S(1)} %iota.4), dimensions={0}, to_apply=%region_1.0 | sort | flops 79872 | bytes 98304 | tf_op jit(solution)/shard_map/jit(argsort)/sort | solution.py:22
  142.3 0.0 copy-start.7
  142.4 34.3 %gather_fusion.1 = f32[6144]{0:T(1024)S(1)} fusion(f32[6144]{0:T(1024)S(1)} %fusion.24, s32[6144]{0:T(1024)S(1)} %fusion.21), kind=kCustom, calls=%fused_computation.1 | custom fusion | bytes 73728 | tf_op jit(solution)/shard_map/gather | solution.py:24
  176.7 0.0 copy-done.7
  176.7 0.2 fusion.8
  176.9 22.4 %all-gather.1 = f32[8,1,128]{2,1,0:T(1,128)S(1)} all-gather(f32[1,1,128]{2,1,0:T(1,128)S(1)} %fusion.8), channel_id=2, replica_groups=mesh['dp'=1,'tp'=4,'ep'=8] {'ep'}, dimensions={0}, use_global_device_ids=true | all-gather | bytes 4608 | tf_op jit(solution)/shard_map/all_gather | solution.py:48
  199.4 0.0 all-gather.4.cloned.1.call-done
  199.4 49.1 %gather_fusion = bf16[6144,2048]{1,0:T(8,128)(2,1)} fusion(bf16[1024,2048]{1,0:T(8,128)(2,1)} %all-gather.4.cloned.1.call-done, s32[6144]{0:T(1024)S(1)} %fusion.23), kind=kCustom, calls=%fused_computation | custom fusion | bytes 50356224 | tf_op jit(solution)/shard_map/jit(_take)/gather | solution.py:26
  248.5 21.7 %broadcast_select_fusion = bf16[6144,2048]{1,0:T(8,128)(2,1)} fusion(bf16[6144,2048]{1,0:T(8,128)(2,1)} %gather_fusion, pred[6144]{0:T(1024)(128)(4,1)S(1)} %get-tuple-element.19), kind=kLoop, calls=%fused_computation.8 | loop fusion | flops 12582912 | bytes 50337792 | tf_op jit(solution)/shard_map/jit(_take)/select_n | solution.py:26
  270.2 16.1 %ragged-dot-none.1 = f32[6144,352]{1,0:T(8,128)} custom-call(s32[1]{0:T(128)} %get-tuple-element.7, s32[9]{0:T(128)} %get-tuple-element.8, s32[31]{0:T(128)} %get-tuple-element.9, s32[31]{0:T(128)} %get-tuple-element.10, s32[1]{0:T(128)} %get-tuple-element.7, bf16[6144,2048]{1,0:T(8,128)(2,1)} %broadcast_select_fusion, bf16[8,2048,352]{2,1,0:T(8,128)(2,1)} %copy.35), custom_call_target="tpu_custom_call" | custom-call | flops 8858370048 | bytes 45350944 | tf_op jit(solution)/shard_map/ragged_dot_general/ragged-dot-none
  286.3 16.1 %ragged-dot-none.2 = f32[6144,352]{1,0:T(8,128)} custom-call(s32[1]{0:T(128)} %get-tuple-element.7, s32[9]{0:T(128)} %get-tuple-element.8, s32[31]{0:T(128)} %get-tuple-element.9, s32[31]{0:T(128)} %get-tuple-element.10, s32[1]{0:T(128)} %get-tuple-element.7, bf16[6144,2048]{1,0:T(8,128)(2,1)} %broadcast_select_fusion, bf16[8,2048,352]{2,1,0:T(8,128)(2,1)} %copy.34), custom_call_target="tpu_custom_call" | custom-call | flops 8858370048 | bytes 45350944 | tf_op jit(solution)/shard_map/ragged_dot_general/ragged-dot-none
  302.4 9.9 %multiply_convert_fusion = bf16[6144,352]{1,0:T(8,128)(2,1)} fusion(f32[6144,352]{1,0:T(8,128)} %ragged-dot-none.1, f32[6144,352]{1,0:T(8,128)} %ragged-dot-none.2), kind=kLoop, calls=%fused_computation.9 | loop fusion | flops 12976128 | bytes 21626880 | tf_op jit(solution)/shard_map/convert_element_type | solution.py:29
  312.2 0.0 copy-start.4
  312.2 0.0 copy-start.3
  312.2 18.5 %ragged-dot-none = f32[6144,2048]{1,0:T(8,128)} custom-call(s32[1]{0:T(128)} %get-tuple-element.7, s32[9]{0:T(128)} %get-tuple-element.8, s32[31]{0:T(128)} %get-tuple-element.9, s32[31]{0:T(128)} %get-tuple-element.10, s32[1]{0:T(128)} %get-tuple-element.7, bf16[6144,352]{1,0:T(8,128)(2,1)} %multiply_convert_fusion, bf16[8,352,2048]{2,1,0:T(8,128)(2,1)} %param.18), custom_call_target="tpu_custom_call" | custom-call | flops 8858370048 | bytes 66191392 | tf_op jit(solution)/shard_map/ragged_dot_general/ragged-dot-none
  330.8 0.0 copy-done.4
  330.8 3.6 fusion.30
  334.4 0.0 copy-done
  334.4 0.0 copy-done.3
  334.4 8.0 %convolution_multiply_fusion = f32[1024,2048]{1,0:T(8,128)} fusion(bf16[88,2048]{1,0:T(8,128)(2,1)S(1)} %copy-done, f32[1024]{0:T(1024)S(1)} %bitcast.31, bf16[1024,2048]{1,0:T(8,128)(2,1)} %all-gather.4.cloned.1.call-done, bf16[2048,88]{0,1:T(8,128)(2,1)S(1)} %copy-done.3, f32[1024,88]{0,1:T(8,128)S(1)} %fusion.30), kind=kOutput, calls=%fused_computation.10 | convolution fusion | flops 740835328 | bytes 13668352 | tf_op jit(solution)/shard_map/dot_general | solution.py:51
  342.4 88.1 %scatter_custom_fusion.1 = f32[1024,2048]{1,0:T(8,128)} fusion(f32[1024,2048]{1,0:T(8,128)} %convolution_multiply_fusion, s32[6144]{0:T(1024)S(1)} %get-tuple-element.20, f32[6144,2048]{1,0:T(8,128)} %ragged-dot-none, f32[6144]{0:T(1024)S(1)} %gather_fusion.1), kind=kCustom, calls=%fused_computation.5 | custom fusion | flops 25165824 | bytes 58744832 | tf_op jit(solution)/shard_map/scatter-add | solution.py:31
  430.5 0.0 copy-start.2
  430.5 6.0 %convert_element_type.30 = bf16[1024,2048]{1,0:T(8,128)(2,1)} convert(f32[1024,2048]{1,0:T(8,128)} %scatter_custom_fusion.1) | non-fusion elementwise | flops 2097152 | bytes 12582912 | tf_op jit(solution)/shard_map/convert_element_type | solution.py:52
  436.5 0.1 reduce-scatter.2.cloned.1.call-update
  436.6 0.1 all-reduce.2.cloned.1.call-start
  436.7 38.5 %reduce-scatter.2.cloned.1.call-done = bf16[128,2048]{1,0:T(8,128)(2,1)} async-done(((bf16[1024,2048]{1,0:T(8,128)(2,1)}), bf16[128,2048]{1,0:T(8,128)(2,1)}) %reduce-scatter.2.cloned.1.call-update) | async-done | bytes 524304 | tf_op jit(solution)/shard_map/reduce_scatter | solution.py:53
  475.2 0.1 all-reduce.2.cloned.1.call-update
  475.2 39.8 %all-reduce.2.cloned.1.call-done = bf16[128,2048]{1,0:T(8,128)(2,1)} async-done(((bf16[128,2048]{1,0:T(8,128)(2,1)}), bf16[128,2048]{1,0:T(8,128)(2,1)}) %all-reduce.2.cloned.1.call-update) | async-done | bytes 524304 | tf_op jit(solution)/shard_map/psum | solution.py:54
  515.1 0.0 copy-done.2
  515.1 2.0 fusion.12
  (14 shorter events, 0.2 us)
Async XLA Ops:
  6.5 327.8 %copy-start = (bf16[88,2048]{1,0:T(8,128)(2,1)S(1)}, bf16[88,2048]{1,0:T(8,128)(2,1)}, u32[]{:S(2)}) copy-start(bf16[88,2048]{1,0:T(8,128)(2,1)} %param.21) | copy-start | bytes 1081348
  6.6 192.9 %all-gather.4.cloned.1.call-start = ((), (), s32[]{:S(2)}) async-start(), calls=%async_computation.1 | async-start | bytes 4718592 | tf_op jit(solution)/shard_map/all_gather | solution.py:45
  10.6 464.5 %reduce-scatter.2.cloned.1.call-start = ((), (), s32[]{:S(2)}) async-start(), calls=%async_computation.2 | async-start | bytes 4718592 | tf_op jit(solution)/shard_map/reduce_scatter | solution.py:53
  92.9 15.4 %copy-start.6 = (s32[128,6]{0,1:T(8,128)S(1)}, s32[128,6]{0,1:T(8,128)}, u32[]{:S(2)}) copy-start(s32[128,6]{0,1:T(8,128)} %param.12) | copy-start | bytes 9220
  92.9 15.6 %copy-start.1 = (bf16[128,2048]{1,0:T(8,128)(2,1)S(1)}, bf16[128,2048]{1,0:T(8,128)(2,1)}, u32[]{:S(2)}) copy-start(bf16[128,2048]{1,0:T(8,128)(2,1)} %fusion.11) | copy-start | bytes 1572868
  92.9 15.6 %copy-start.5 = (bf16[2048,64]{0,1:T(8,128)(2,1)S(1)}, bf16[2048,64]{0,1:T(8,128)(2,1)}, u32[]{:S(2)}) copy-start(bf16[2048,64]{0,1:T(8,128)(2,1)} %param.14) | copy-start | bytes 786436
  142.3 34.3 %copy-start.7 = (bf16[2048,1]{0,1:T(2,128)(2,1)S(1)}, bf16[2048,1]{0,1:T(2,128)(2,1)}, u32[]{:S(2)}) copy-start(bf16[2048,1]{0,1:T(2,128)(2,1)} %param.15) | copy-start | bytes 12292
  312.2 18.5 %copy-start.4 = (bf16[2048,88]{0,1:T(8,128)(2,1)S(1)}, bf16[2048,88]{0,1:T(8,128)(2,1)}, u32[]{:S(2)}) copy-start(bf16[2048,88]{0,1:T(8,128)(2,1)} %param.19) | copy-start | bytes 1081348
  312.2 22.1 %copy-start.3 = (bf16[2048,88]{0,1:T(8,128)(2,1)S(1)}, bf16[2048,88]{0,1:T(8,128)(2,1)}, u32[]{:S(2)}) copy-start(bf16[2048,88]{0,1:T(8,128)(2,1)} %param.20) | copy-start | bytes 1081348
  430.5 84.6 %copy-start.2 = (bf16[128,2048]{1,0:T(8,128)(2,1)S(1)}, bf16[128,2048]{1,0:T(8,128)(2,1)}, u32[]{:S(2)}) copy-start(bf16[128,2048]{1,0:T(8,128)(2,1)} %param.11) | copy-start | bytes 1572868
  436.6 78.5 %all-reduce.2.cloned.1.call-start = ((), (), s32[]{:S(2)}) async-start(), calls=%async_computation.3 | async-start | bytes 1048576 | tf_op jit(solution)/shard_map/psum | solution.py:54
Sparse Core Ops, SparseCore 0:
  10.7 33.8 all-gather.3
  436.7 38.4 reduce-scatter.1
  477.5 37.4 all-reduce.1
where the time goes:
time: 525 us; the launch traced here: 524 us
  other arithmetic  182 us (35%)
  local copies, waits for them, and re-layouts  122 us (23%)
  waiting for transfers between devices  78.5 us (15%)
  blocking collectives  63.1 us (12%)
  Pallas kernels  52.3 us (10%)
  between operations  13.3 us (3%)
  matrix products  12.1 us (2%)
    scatter-add x1, other arithmetic, routed_part(): jax.ops.segment_sum(down_val * row_wts[:, None], tok_ids, num_segments=n_...  88.1 us
    another operation x3, Pallas kernels  50.6 us
    gather x1, local copies, waits for them, and re-layouts, routed_part(): rows = jnp.take(all_h, tok_ids, axis=0)  49.1 us
    scatter-add x1, other arithmetic, routed_part(): jax.ops.segment_sum(jnp.ones_like(sort_key), sort_key, num_segments=n_loc...  43.5 us
    psum x1, waiting for transfers between devices, local_step(): total = lax.psum(own_rows, 'tp')  39.8 us
    reduce_scatter x1, waiting for transfers between devices, local_step(): lax.psum_scatter(partial_sum, 'ep', scatter_dimension=0, tiled=True)  38.5 us
    gather x1, local copies, waits for them, and re-layouts, routed_part(): row_wts = jnp.where(is_local, all_wt.reshape(-1), 0.0)[order]  34.3 us
    unnamed x18, local copies, waits for them, and re-layouts  31.6 us
  transfers between devices with their start and end apart: 3, of which 2 were waited for; matrix products, arithmetic and copies ran while one was open for 24% of the time, Pallas kernels for 0%

commit v1 on v0

v1 whole, which is shorter than its diff:
```python
import functools

import jax
import jax.numpy as jnp
from jax import lax
from jax.experimental import pallas as pl
from jax.experimental.pallas import tpu as pltpu
from jax.sharding import PartitionSpec as P

RMS_EPS = 1e-6
LANES = 128
PITCH = 24
TILES = (64, 256, 320, 384, 512)
SLOTS = 3
F32 = jnp.float32
BF16 = jnp.bfloat16


def router_columns(rw_ref, sig_ref, out_ref):
    n_exp = rw_ref.shape[1]
    out_ref[...] = jnp.zeros_like(out_ref)
    out_ref[:, :n_exp] = rw_ref[...]
    lane = lax.broadcasted_iota(jnp.int32, (256, LANES), 1)

    def put(step, carry):
        rows = pl.ds(pl.multiple_of(step * 256, 256), 256)
        sig = sig_ref[rows, :].astype(F32)
        out_ref[rows, :] = jnp.where(lane == n_exp, sig, out_ref[rows, :].astype(F32)).astype(BF16)
        return carry

    lax.fori_loop(0, out_ref.shape[0] // 256, put, 0)


def token_block(x, gain, rcol_ref, shg_ref, shu_ref, n_exp):
    xf = x.astype(F32)
    inv = lax.rsqrt(jnp.mean(xf * xf, axis=-1, keepdims=True) + RMS_EPS)
    h = (xf * inv * gain.astype(F32)).astype(BF16)
    logits = jnp.dot(h, rcol_ref[...], preferred_element_type=F32)
    lane = lax.broadcasted_iota(jnp.int32, logits.shape, 1)
    masked = jnp.where(lane < n_exp, logits, -jnp.inf)
    top = jnp.max(masked, axis=-1, keepdims=True)
    ex = jnp.exp(masked - top)
    prob = ex / jnp.sum(ex, axis=-1, keepdims=True)
    sig = jax.nn.sigmoid(logits[:, n_exp:n_exp + 1])
    gate = jnp.dot(h, shg_ref[...], preferred_element_type=F32)
    up = jnp.dot(h, shu_ref[...], preferred_element_type=F32)
    act = (jax.nn.silu(gate) * up).astype(BF16)
    return h, prob.T, sig, act


def routing_lists(idx_t, wt, first, n_local, lst_ref, wl_ref, cnt_ref):
    n_tok = idx_t.shape[1]
    n_hi = n_tok // LANES
    sub = lax.broadcasted_iota(jnp.int32, (n_local, n_tok), 0)
    member = jnp.zeros((n_local, n_tok), F32)
    for e in range(n_local):
        hit = jnp.sum((idx_t == first + e).astype(F32), axis=0, keepdims=True)
        member = jnp.where(sub == e, hit, member)
    tri = (lax.broadcasted_iota(jnp.int32, (LANES, LANES), 0)
           < lax.broadcasted_iota(jnp.int32, (LANES, LANES), 1)).astype(BF16)
    base = jnp.zeros((n_local, 1), F32)
    parts = []
    for b in range(n_hi):
        m_b = member[:, b * LANES:(b + 1) * LANES]
        parts.append(jnp.dot(m_b.astype(BF16), tri, preferred_element_type=F32) + base)
        base = base + jnp.sum(m_b, axis=-1, keepdims=True)
    pos = jnp.concatenate(parts, axis=1).astype(jnp.int32)
    cnt_ref[...] = jnp.broadcast_to(base, cnt_ref.shape).astype(jnp.int32)
    tok = lax.broadcasted_iota(jnp.int32, (n_hi, n_tok), 1)
    hi_id = lax.broadcasted_iota(jnp.int32, (n_hi, n_tok), 0)
    lo_id = lax.broadcasted_iota(jnp.int32, (LANES, n_tok), 0)
    row_id = (lax.broadcasted_iota(jnp.int32, (n_hi, LANES), 0) * LANES
              + lax.broadcasted_iota(jnp.int32, (n_hi, LANES), 1))
    tok_hi = (tok // 8).astype(F32)
    tok_lo = (tok % 8).astype(F32)
    for e in range(n_local):
        p_e = pos[e:e + 1, :]
        here = ((p_e // LANES) == hi_id) & (member[e:e + 1, :] > 0.0)
        lo_hot = jnp.where((p_e % LANES) == lo_id, 1.0, 0.0).astype(BF16)
        w = wt[e:e + 1, :]
        w1 = w.astype(BF16).astype(F32)
        w2 = (w - w1).astype(BF16).astype(F32)
        w3 = w - w1 - w2
        rows = [jnp.where(here, v, 0.0) for v in (tok_hi, tok_lo, w1, w2, w3)]
        lhs = jnp.concatenate(rows, axis=0).astype(BF16)
        got = lax.dot_general(lhs, lo_hot, (((1,), (1,)), ((), ())), preferred_element_type=F32)
        t_of = got[:n_hi] * 8.0 + got[n_hi:2 * n_hi]
        w_of = (got[2 * n_hi:3 * n_hi] + got[3 * n_hi:4 * n_hi]) + got[4 * n_hi:]
        valid = row_id < base[e:e + 1, :].astype(jnp.int32)
        lst_ref[e * n_hi:(e + 1) * n_hi, :] = jnp.where(valid, t_of.astype(jnp.int32), n_tok)
        wl_ref[e * n_hi:(e + 1) * n_hi, :] = jnp.where(valid, w_of, 0.0)


def prep_kernel(n_local, x_ref, idx_ref, gain_ref, rw_ref, sig_ref, shg_ref, shu_ref,
                h_ref, act_ref, sigv_ref, lst_ref, wl_ref, cnt_ref, rcol, probs):
    n_exp = rw_ref.shape[1]
    router_columns(rw_ref, sig_ref, rcol)
    n_blocks = x_ref.shape[0] // LANES

    def block(b, carry):
        rows = pl.ds(pl.multiple_of(b * LANES, LANES), LANES)
        h, prob_t, sig, act = token_block(x_ref[rows, :], gain_ref[...], rcol, shg_ref, shu_ref, n_exp)
        h_ref[rows, :] = h
        probs[b] = prob_t
        sigv_ref[rows, :] = sig
        act_ref[rows, :] = act
        return carry

    lax.fori_loop(0, n_blocks, block, 0)
    first = pl.multiple_of(lax.axis_index("ep") * n_local, n_local)
    wt = jnp.concatenate([probs[b, pl.ds(first, n_local), :] for b in range(n_blocks)], axis=1)
    routing_lists(idx_ref[...], wt, first, n_local, lst_ref, wl_ref, cnt_ref)


def expert_kernel(lst, wl, cnt, h_hbm, act_ref, sig_ref, shd_ref, wg_hbm, wu_hbm, wd_hbm, out_hbm,
                  h_in, table, acc, wg, wu, wd, xt, xb, fb, ob, active, in_sem, w_sem, out_sem):
    n_tok, dim = h_hbm.shape
    n_local = wg_hbm.shape[0]
    n_chunk = dim // LANES
    n_blocks = n_tok // LANES

    def fetch_h(b):
        return pltpu.make_async_copy(h_hbm.at[pl.ds(b * LANES, LANES), :], h_in.at[b], in_sem.at[b])

    def weight_copies(e, s):
        return (pltpu.make_async_copy(wg_hbm.at[e], wg.at[s], w_sem.at[s, 0]),
                pltpu.make_async_copy(wu_hbm.at[e], wu.at[s], w_sem.at[s, 1]),
                pltpu.make_async_copy(wd_hbm.at[e], wd.at[s], w_sem.at[s, 2]))

    for b in range(n_blocks):
        fetch_h(b).start()

    def note(e, n):
        has = cnt[e, 0] > 0

        @pl.when(has)
        def _():
            active[n] = e

        return n + jnp.where(has, 1, 0)

    n_active = lax.fori_loop(0, n_local, note, 0)
    for s in range(SLOTS - 1):
        @pl.when(s < n_active)
        def _():
            for c in weight_copies(active[s], s):
                c.start()

    def clear(i, carry):
        acc[pl.ds(pl.multiple_of(i * 128, 128), 128), :] = jnp.zeros((128, LANES), F32)
        return carry

    lax.fori_loop(0, (n_tok * PITCH) // 128, clear, 0)
    acc[n_tok * PITCH:, :] = jnp.zeros((acc.shape[0] - n_tok * PITCH, LANES), F32)
    table[n_tok * PITCH:, :] = jnp.zeros((table.shape[0] - n_tok * PITCH, LANES), F32)

    def spread(b, carry):
        fetch_h(b).wait()
        for c in range(n_chunk):
            table[pl.ds(b * LANES * PITCH + c, LANES, stride=PITCH), :] = (
                h_in[b, :, c * LANES:(c + 1) * LANES].astype(F32))
        return carry

    lax.fori_loop(0, n_blocks, spread, 0)

    def rows_of(e, r):
        return lst[e * n_blocks + r // LANES, r % LANES]

    def ffn(m, e, s, r0, n):
        stride = m + 8
        groups = (n + 7) // 8

        def gather(g, carry):
            for i in range(8):
                r = g * 8 + i
                t = rows_of(e, r0 + r)
                slab = table[pl.ds(pl.multiple_of(t * PITCH, 8), n_chunk), :]
                xt[pl.ds(r, n_chunk, stride=stride), :] = slab
            return carry

        lax.fori_loop(0, groups, gather, 0)
        for c in range(n_chunk):
            xb[:m, c * LANES:(c + 1) * LANES] = xt[c * stride:c * stride + m, :].astype(BF16)
        gate = jnp.dot(xb[:m, :], wg[s], preferred_element_type=F32)
        up = jnp.dot(xb[:m, :], wu[s], preferred_element_type=F32)
        act = (jax.nn.silu(gate) * up).astype(BF16)
        for c in range(0, n_chunk, 2):
            f = jnp.dot(act, wd[s, :, c * LANES:(c + 2) * LANES], preferred_element_type=F32)
            fb[c * stride:c * stride + m, :] = f[:, :LANES]
            fb[(c + 1) * stride:(c + 1) * stride + m, :] = f[:, LANES:]

        def scatter(g, carry):
            where, old, new = [], [], []
            for i in range(8):
                r = g * 8 + i
                t = rows_of(e, r0 + r)
                where.append(pl.multiple_of(t * PITCH, 8))
                old.append(acc[pl.ds(where[i], n_chunk), :])
            for i in range(8):
                r = g * 8 + i
                w = wl[e * n_blocks + (r0 + r) // LANES, (r0 + r) % LANES]
                new.append(old[i] + w * fb[pl.ds(r, n_chunk, stride=stride), :])
            for i in range(8):
                acc[pl.ds(where[i], n_chunk), :] = new[i]
            return carry

        lax.fori_loop(0, groups, scatter, 0)

    big = TILES[-1]

    def expert(i, carry):
        e = active[i]
        s = lax.rem(i, SLOTS)
        ahead = i + SLOTS - 1

        @pl.when(ahead < n_active)
        def _():
            for c in weight_copies(active[ahead], lax.rem(ahead, SLOTS)):
                c.start()

        for c in weight_copies(e, s):
            c.wait()
        total = cnt[e, 0]

        def piece(j, carry2):
            r0 = j * big
            n = jnp.minimum(total - r0, big)
            below = 0
            for m in TILES:
                @pl.when((n > below) & (n <= m))
                def _(m=m):
                    ffn(m, e, s, r0, n)
                below = m
            return carry2

        lax.fori_loop(0, (total + big - 1) // big, piece, 0)
        return carry

    lax.fori_loop(0, n_active, expert, 0)

    def write_out(b, slot):
        return pltpu.make_async_copy(ob.at[slot], out_hbm.at[pl.ds(b * LANES, LANES), :], out_sem.at[slot])

    def finish(b, carry):
        slot = lax.rem(b, 2)

        @pl.when(b >= 2)
        def _():
            write_out(b - 2, slot).wait()

        rows = pl.ds(pl.multiple_of(b * LANES, LANES), LANES)
        sig = sig_ref[rows, :]
        for c in range(0, n_chunk, 2):
            sh = sig * jnp.dot(act_ref[rows, :], shd_ref[:, c * LANES:(c + 2) * LANES], preferred_element_type=F32)
            for d in range(2):
                routed = acc[pl.ds(b * LANES * PITCH + c + d, LANES, stride=PITCH), :]
                ob[slot, :, (c + d) * LANES:(c + d + 1) * LANES] = (
                    routed + sh[:, d * LANES:(d + 1) * LANES]).astype(BF16)
        write_out(b, slot).start()
        return carry

    lax.fori_loop(0, n_blocks, finish, 0)
    for b in (n_blocks - 2, n_blocks - 1):
        write_out(b, b % 2).wait()


def run_experts(lst, wl, cnt, h, act, sig, shd, wg, wu, wd):
    n_tok, dim = h.shape
    n_local, _, width = wg.shape
    n_chunk = dim // LANES
    big = TILES[-1]
    smem = pl.BlockSpec(memory_space=pltpu.SMEM)
    vmem = pl.BlockSpec(memory_space=pltpu.VMEM)
    hbm = pl.BlockSpec(memory_space=pl.ANY)
    return pl.pallas_call(
        expert_kernel,
        out_shape=jax.ShapeDtypeStruct((n_tok, dim), BF16),
        in_specs=[smem] * 3 + [hbm] + [vmem] * 3 + [hbm] * 3,
        out_specs=hbm,
        scratch_shapes=[
            pltpu.VMEM((n_tok // LANES, LANES, dim), BF16),
            pltpu.VMEM(((n_tok + 1) * PITCH, LANES), F32),
            pltpu.VMEM(((n_tok + 1) * PITCH, LANES), F32),
            pltpu.VMEM((SLOTS, dim, width), BF16),
            pltpu.VMEM((SLOTS, dim, width), BF16),
            pltpu.VMEM((SLOTS, width, dim), BF16),
            pltpu.VMEM((n_chunk * (big + 8), LANES), F32),
            pltpu.VMEM((big, dim), BF16),
            pltpu.VMEM((n_chunk * (big + 8), LANES), F32),
            pltpu.VMEM((2, LANES, dim), BF16),
            pltpu.SMEM((n_local,), jnp.int32),
            pltpu.SemaphoreType.DMA((n_tok // LANES,)),
            pltpu.SemaphoreType.DMA((SLOTS, 3)),
            pltpu.SemaphoreType.DMA((2,)),
        ],
        compiler_params=pltpu.CompilerParams(vmem_limit_bytes=64 * 1000 * 1000),
        name="experts",
    )(lst, wl, cnt, h, act, sig, shd, wg, wu, wd)


def solution(mesh):
    tok_spec = P(('dp', 'ep'), None)
    in_specs = (tok_spec, tok_spec, P(None), P(None, None), P(None, None),
                P('ep', None, 'tp'), P('ep', None, 'tp'), P('ep', 'tp', None),
                P(None, ('tp', 'ep')), P(None, ('tp', 'ep')), P(('tp', 'ep'), None))

    def local_step(hidden_in, topk_idx, norm_gain, router_w, shared_sig_w, exp_gate, exp_up, exp_down,
                   sh_gate, sh_up, sh_down):
        n_local = exp_gate.shape[0]
        dim = hidden_in.shape[1]
        all_x = lax.all_gather(hidden_in, 'ep', axis=0, tiled=True)
        idx_t = jnp.pad(topk_idx.T, ((0, 8 - topk_idx.shape[1]), (0, 0)), constant_values=-1)
        all_idx = lax.all_gather(idx_t, 'ep', axis=1, tiled=True)
        n_tok = all_x.shape[0]
        n_hi = n_tok // LANES
        h, act, sig, lst, wl, cnt = pl.pallas_call(
            functools.partial(prep_kernel, n_local),
            out_shape=(jax.ShapeDtypeStruct((n_tok, dim), BF16),
                       jax.ShapeDtypeStruct((n_tok, sh_gate.shape[1]), BF16),
                       jax.ShapeDtypeStruct((n_tok, 1), F32),
                       jax.ShapeDtypeStruct((n_local * n_hi, LANES), jnp.int32),
                       jax.ShapeDtypeStruct((n_local * n_hi, LANES), F32),
                       jax.ShapeDtypeStruct((n_local, LANES), jnp.int32)),
            in_specs=[pl.BlockSpec(memory_space=pltpu.VMEM)] * 7,
            out_specs=[pl.BlockSpec(memory_space=pltpu.VMEM)] * 6,
            scratch_shapes=[pltpu.VMEM((dim, LANES), BF16), pltpu.VMEM((n_hi, LANES, LANES), F32)],
            name="prep",
        )(all_x, all_idx, norm_gain.reshape(1, -1), router_w, shared_sig_w, sh_gate, sh_up)
        partial = run_experts(lst, wl, cnt, h, act, sig, sh_down, exp_gate, exp_up, exp_down)
        own_rows = lax.psum_scatter(partial, 'ep', scatter_dimension=0, tiled=True)
        total = lax.psum(own_rows, 'tp')
        return (hidden_in.astype(F32) + total.astype(F32)).astype(BF16)

    return jax.shard_map(local_step, mesh=mesh, in_specs=in_specs, out_specs=tok_spec, check_vma=False)
```

time: 525 us -> 212 us (0.40)
  other arithmetic: 182 us -> 1.96 us
  local copies, waits for them, and re-layouts: 122 us -> 40 us
  blocking collectives: 63.1 us -> 19 us
  waiting for transfers between devices: 78.5 us -> 103 us
  Pallas kernels: 52.3 us -> 35.1 us
  matrix products: 12.1 us -> 0 us
    scatter-add x2 -> x0, other arithmetic: 132 us -> none  [the longest x1 88.1 us: routed_part(): jax.ops.segment_sum(down_val * row_wts[:, None], tok_ids, num_segments=n_...]
    gather x7 -> x0, local copies, waits for them, and re-layouts: 88.9 us -> none  [the longest x1 49.1 us: routed_part(): rows = jnp.take(all_h, tok_ids, axis=0)]
    another operation x3 -> x0, Pallas kernels: 50.6 us -> none
    all_gather x3 -> x1, blocking collectives: 63.1 us -> 19 us  [local_step(): all_idx = lax.all_gather(idx_t, 'ep', axis=1, tiled=True)]
    pallas_call x0 -> x2, Pallas kernels: none -> 35.1 us  [the longest x1 23.3 us: run_experts(): pl.pallas_call(expert_kernel, out_shape=jax.ShapeDtypeStruct((n_tok, dim)...]
    reduce_scatter x1, waiting for transfers between devices: 38.5 us -> 61.9 us  [local_step(): own_rows = lax.psum_scatter(partial, 'ep', scatter_dimension=0, tiled=True)]
    select_n x5 -> x0, other arithmetic: 21.8 us -> none  [the longest x1 21.7 us: routed_part(): rows = jnp.take(all_h, tok_ids, axis=0)]
    convert_element_type x5 -> x1, other arithmetic: 20.6 us -> 1.96 us  [local_step(): return (hidden_in.astype(F32) + total.astype(F32)).astype(BF16)]
  transfers between devices with their start and end apart: 3 -> 3, of which waited for: 2 -> 2; matrix products, arithmetic and copies ran while one was open for 24% -> 19% of each run, Pallas kernels for 0% -> 0%
where the time goes in v1:
time: 212 us
  waiting for transfers between devices  103 us (49%)
  local copies, waits for them, and re-layouts  40 us (19%)
  Pallas kernels  35.1 us (17%)
  blocking collectives  19 us (9%)
  between operations  13.1 us (6%)
    reduce_scatter x1, waiting for transfers between devices, local_step(): own_rows = lax.psum_scatter(partial, 'ep', scatter_dimension=0, tiled=True)  61.9 us
    psum x1, waiting for transfers between devices, local_step(): total = lax.psum(own_rows, 'tp')  39.8 us
    unnamed x10, local copies, waits for them, and re-layouts  38.7 us
    pallas_call x1, Pallas kernels, run_experts(): pl.pallas_call(expert_kernel, out_shape=jax.ShapeDtypeStruct((n_tok, dim)...  23.3 us
    all_gather x1, blocking collectives, local_step(): all_idx = lax.all_gather(idx_t, 'ep', axis=1, tiled=True)  19 us
    pallas_call x1, Pallas kernels, local_step(): pl.pallas_call(functools.partial(prep_kernel, n_local), out_shape=(jax.Sh...  11.8 us
  transfers between devices with their start and end apart: 3, of which 2 were waited for; matrix products, arithmetic and copies ran while one was open for 19% of the time, Pallas kernels for 0%

profile of v1, /device:TPU:97, one launch (start us, length us, event | category | flops | bytes accessed | tf_op | source)
XLA Modules:
  0.0 211.8 jit_solution(2436388962836382166)
XLA Ops:
  6.5 0.0 all-gather.2.cloned.1.call-start
  6.6 0.7 all-gather.2.cloned.1.call-update
  7.3 0.1 reduce-scatter.2.cloned.1.call-start
  7.4 1.3 reshape.3.gain_ref
  8.7 2.0 copy.12.rw_ref
  10.6 1.8 copy.13.sig_ref
  12.4 2.0 copy.14.shg_ref
  14.4 2.0 copy.15.shu_ref
  16.4 15.7 %copy.16.wg_hbm = bf16[8,2048,352]{2,1,0:T(8,128)(2,1)} copy(bf16[8,2048,352]{1,2,0:T(8,128)(2,1)} %param.16) | data formatting | bytes 23068672 | tf_op args[5]
  32.1 0.0 copy-start.1
  32.1 15.3 %copy.17.wu_hbm = bf16[8,2048,352]{2,1,0:T(8,128)(2,1)} copy(bf16[8,2048,352]{1,2,0:T(8,128)(2,1)} %param.17) | data formatting | bytes 23068672 | tf_op args[6]
  47.4 0.0 copy-done.1
  47.4 19.0 %all_gather.7.idx_ref = s32[8,1024]{1,0:T(8,128)} all-gather(s32[8,128]{1,0:T(8,128)S(1)} %pad.4), channel_id=1, replica_groups=mesh['dp'=1,'tp'=4,'ep'=8] {'ep'}, dimensions={1}, use_global_device_ids=true | all-gather | bytes 36864 | tf_op jit(solution)/shard_map/all_gather | solution.py:313
  66.3 0.0 all-gather.2.cloned.1.call-done.x_ref
  66.3 11.8 %prep.1 = (bf16[1024,2048]{1,0:T(8,128)(2,1)}, bf16[1024,88]{1,0:T(8,128)(2,1)}, f32[1024,1]{1,0:T(8,128)}, s32[64,128]{1,0:T(8,128)}, f32[64,128]{1,0:T(8,128)}, /*index=5*/s32[8,128]{1,0:T(8,128)}) custom-call(bf16[1024,2048]{1,0:T(8,128)(2,1)} %all-gather.2.cloned.1.call-done.x_ref, s32[8,1024]{1,0:T(8,128)} %all_gather.7.idx_ref, ...), custom_call_target="tpu_custom_call" | custom-call | tf_op jit(solution)/shard_map/prep/pallas_call | solution.py:316
  78.1 0.0 copy-start
  78.1 23.3 %experts.1 = bf16[1024,2048]{1,0:T(8,128)(2,1)} custom-call(s32[64,128]{1,0:T(8,128)} %get-tuple-element.11.lst, f32[64,128]{1,0:T(8,128)} %get-tuple-element.12.wl, s32[8,128]{1,0:T(8,128)} %get-tuple-element.13.cnt, bf16[1024,2048]{1,0:T(8,128)(2,1)} %get-tuple-element.14.h_hbm, bf16[1024,88]{1,0:T(8,128)(2,1)} %get-tuple-element.15.act_ref, ...), custom_call_target="tpu_custom_call" | custom-call | tf_op jit(solution)/shard_map/experts/pallas_call | solution.py:275
  101.4 0.1 reduce-scatter.2.cloned.1.call-update
  101.5 0.1 all-reduce.3.cloned.1.call-start
  101.6 61.9 %reduce-scatter.2.cloned.1.call-done = bf16[128,2048]{1,0:T(8,128)(2,1)} async-done(((bf16[1024,2048]{1,0:T(8,128)(2,1)}), bf16[128,2048]{1,0:T(8,128)(2,1)}) %reduce-scatter.2.cloned.1.call-update) | async-done | bytes 524304 | tf_op jit(solution)/shard_map/reduce_scatter | solution.py:330
  163.5 0.1 all-reduce.3.cloned.1.call-update
  163.5 39.8 %all-reduce.3.cloned.1.call-done = bf16[128,2048]{1,0:T(8,128)(2,1)} async-done(((bf16[128,2048]{1,0:T(8,128)(2,1)}), bf16[128,2048]{1,0:T(8,128)(2,1)}) %all-reduce.3.cloned.1.call-update) | async-done | bytes 524304 | tf_op jit(solution)/shard_map/psum | solution.py:331
  203.3 0.0 copy-done
  203.3 2.0 add_convert_fusion
  (1 shorter events, 0.0 us)
Async XLA Ops:
  6.5 59.8 %all-gather.2.cloned.1.call-start = ((), (), s32[]{:S(2)}) async-start(), calls=%async_computation.1 | async-start | bytes 4718592 | tf_op jit(solution)/shard_map/all_gather | solution.py:311
  7.3 156.2 %reduce-scatter.2.cloned.1.call-start = ((), (), s32[]{:S(2)}) async-start(), calls=%async_computation.2 | async-start | bytes 4718592 | tf_op jit(solution)/shard_map/reduce_scatter | solution.py:330
  32.1 15.3 %copy-start.1 = (s32[128,6]{0,1:T(8,128)S(1)}, s32[128,6]{0,1:T(8,128)}, u32[]{:S(2)}) copy-start(s32[128,6]{0,1:T(8,128)} %param.12) | copy-start | bytes 9220
  78.1 125.2 %copy-start = (bf16[128,2048]{1,0:T(8,128)(2,1)S(1)}, bf16[128,2048]{1,0:T(8,128)(2,1)}, u32[]{:S(2)}) copy-start(bf16[128,2048]{1,0:T(8,128)(2,1)} %param.11) | copy-start | bytes 1572868
  101.5 101.8 %all-reduce.3.cloned.1.call-start = ((), (), s32[]{:S(2)}) async-start(), calls=%async_computation.3 | async-start | bytes 1048576 | tf_op jit(solution)/shard_map/psum | solution.py:331
Sparse Core Ops, SparseCore 0:
  9.0 33.5 all-gather.1
  101.6 61.7 reduce-scatter.1
  165.8 37.4 all-reduce.2

commit v2 on v1

v2 whole, which is shorter than its diff:
```python
import functools

import jax
import jax.numpy as jnp
from jax import lax
from jax.experimental import pallas as pl
from jax.experimental.pallas import tpu as pltpu
from jax.sharding import PartitionSpec as P

RMS_EPS = 1e-6
LANES = 128
PITCH = 24
TILES = (64, 256, 320, 384, 512)
SLOTS = 3
F32 = jnp.float32
BF16 = jnp.bfloat16
NT = (((1,), (1,)), ((), ()))
TN = (((0,), (0,)), ((), ()))
MESH = pl.DeviceIdType.MESH


def place():
    ep, y = lax.axis_index("ep"), lax.axis_index("tp")
    return ep // 2, ep % 2, y, lax.axis_size("ep") // 2, lax.axis_size("tp")


def peer(x, core, y):
    return {"ep": 2 * x + core, "tp": y}


def remote(src, dst, send, recv, where):
    return pltpu.make_async_remote_copy(src_ref=src, dst_ref=dst, send_sem=send, recv_sem=recv,
                                        device_id=where, device_id_type=MESH)


def meet(peers):
    barrier = pltpu.get_barrier_semaphore()
    for p in peers:
        pl.semaphore_signal(barrier, inc=1, device_id=p, device_id_type=MESH)
    pl.semaphore_wait(barrier, len(peers))


def token_pair(x, gain, sigw, cols_ref, n_exp, width, up_at):
    xf = x.astype(F32)
    inv = lax.rsqrt(jnp.mean(xf * xf, axis=-1, keepdims=True) + RMS_EPS)
    h = (xf * inv * gain.astype(F32)).astype(BF16)
    sig = jax.nn.sigmoid(jnp.sum(h.astype(F32) * sigw.astype(F32), axis=-1, keepdims=True))
    return h, sig


def pair_dots(h, cols_ref, n_exp, width, up_at):
    out = lax.dot_general(cols_ref[...], h, NT, preferred_element_type=F32)
    logits = out[:n_exp]
    ex = jnp.exp(logits - jnp.max(logits, axis=0, keepdims=True))
    prob = ex / jnp.sum(ex, axis=0, keepdims=True)
    act = (jax.nn.silu(out[n_exp:n_exp + width]) * out[up_at:up_at + width]).astype(BF16)
    return prob, act


def routing_lists(idx_t, wt, first, n_local, lst_ref, wl_ref, cnt_ref):
    n_tok = idx_t.shape[1]
    n_hi = n_tok // LANES
    sub = lax.broadcasted_iota(jnp.int32, (n_local, n_tok), 0)
    member = jnp.zeros((n_local, n_tok), F32)
    for e in range(n_local):
        hit = jnp.sum((idx_t == first + e).astype(F32), axis=0, keepdims=True)
        member = jnp.where(sub == e, hit, member)
    tri = (lax.broadcasted_iota(jnp.int32, (LANES, LANES), 0)
           < lax.broadcasted_iota(jnp.int32, (LANES, LANES), 1)).astype(F32).astype(BF16)
    base = jnp.zeros((n_local, 1), F32)
    parts = []
    for b in range(n_hi):
        m_b = member[:, b * LANES:(b + 1) * LANES]
        parts.append(jnp.dot(m_b.astype(BF16), tri, preferred_element_type=F32) + base)
        base = base + jnp.sum(m_b, axis=-1, keepdims=True)
    pos = jnp.concatenate(parts, axis=1).astype(jnp.int32)
    cnt_ref[...] = jnp.broadcast_to(base, cnt_ref.shape).astype(jnp.int32)
    tok = lax.broadcasted_iota(jnp.int32, (n_hi, n_tok), 1)
    hi_id = lax.broadcasted_iota(jnp.int32, (n_hi, n_tok), 0)
    lo_id = lax.broadcasted_iota(jnp.int32, (LANES, n_tok), 0)
    row_id = (lax.broadcasted_iota(jnp.int32, (n_hi, LANES), 0) * LANES
              + lax.broadcasted_iota(jnp.int32, (n_hi, LANES), 1))
    tok_hi = (tok >> 3).astype(F32)
    tok_lo = (tok & 7).astype(F32)
    for e in range(n_local):
        p_e = pos[e:e + 1, :]
        here = ((p_e >> 7) == hi_id) & (member[e:e + 1, :] > 0.0)
        lo_hot = jnp.where((p_e & (LANES - 1)) == lo_id, 1.0, 0.0).astype(BF16)
        w = wt[e:e + 1, :]
        w1 = w.astype(BF16).astype(F32)
        w2 = (w - w1).astype(BF16).astype(F32)
        w3 = w - w1 - w2
        rows = [jnp.where(here, v, 0.0) for v in (tok_hi, tok_lo, w1, w2, w3)]
        lhs = jnp.concatenate(rows, axis=0).astype(BF16)
        got = lax.dot_general(lhs, lo_hot, NT, preferred_element_type=F32)
        t_of = got[:n_hi] * 8.0 + got[n_hi:2 * n_hi]
        w_of = (got[2 * n_hi:3 * n_hi] + got[3 * n_hi:4 * n_hi]) + got[4 * n_hi:]
        valid = row_id < base[e:e + 1, :].astype(jnp.int32)
        lst_ref[e * n_hi:(e + 1) * n_hi, :] = jnp.where(valid, t_of.astype(jnp.int32), n_tok) * PITCH
        wl_ref[e * n_hi:(e + 1) * n_hi, :] = jnp.where(valid, w_of, 0.0)


def gather_kernel(n_local, x_hbm, idx_hbm, gain_ref, rw_ref, sigw_ref, shg_ref, shu_ref,
                  h_hbm, act_ref, sigv_ref, lst_ref, wl_ref, cnt_ref,
                  tok, idx, cols, prob, hbuf, in_sem, send, recv, isend, irecv, out_sem):
    x, core, y, n_x, n_y = place()
    n_exp, width = rw_ref.shape[0], shg_ref.shape[0]
    up_at = n_exp + (width + 15) // 16 * 16
    rows = x_hbm.shape[0]
    half, piece = rows // 2, rows // 4
    own = 2 * x + core
    load_x = pltpu.make_async_copy(x_hbm, tok.at[own], in_sem.at[0])
    load_i = pltpu.make_async_copy(idx_hbm, idx.at[own], in_sem.at[1])
    load_x.start()
    load_i.start()

    def at(v, n):
        return lax.rem(v + n, n)

    right, left, far = at(x + 1, n_x), at(x - 1, n_x), at(x + 2, n_x)
    up, down = at(y + 1, n_y), at(y - 1, n_y)
    others = [peer(x, 1 - core, y)]
    for d in (right, left, far):
        for c in (core, 1 - core):
            others.append(peer(d, c, y))
    meet(others + [peer(x, core, up), peer(x, core, down)])
    load_x.wait()
    load_i.wait()

    started = []
    count = [0]

    def copy(block, row, n_rows, where):
        k = count[0]
        count[0] += 1
        row = pl.multiple_of(row, piece)
        ref = tok.at[block, pl.ds(row, n_rows), :]
        c = remote(ref, ref, send.at[k], recv.at[k], where)
        return c

    def go(c):
        c.start()
        started.append(c)
        return c

    mine = (y % 2) * half
    m0, m1 = mine, mine + piece
    to_right, to_left = peer(right, core, y), peer(left, core, y)
    to_up, to_down, to_mate = peer(x, core, up), peer(x, core, down), peer(x, 1 - core, y)
    s_r0 = go(copy(own, m0, piece, to_right))
    s_l1 = go(copy(own, m1, piece, to_left))
    s_mate = go(copy(own, 0, rows, to_mate))
    s_r1 = go(copy(own, m1, piece, to_right))
    s_l0 = go(copy(own, m0, piece, to_left))
    icopies = []
    for k, p in enumerate(others):
        c = remote(idx.at[own], idx.at[own], isend.at[k], irecv.at[k], p)
        c.start()
        icopies.append(c)

    cols[...] = jnp.zeros_like(cols)
    cols[:n_exp, :] = rw_ref[...]
    cols[n_exp:n_exp + width, :] = shg_ref[...]
    cols[up_at:up_at + width, :] = shu_ref[...]

    outs = []

    def pair(slot, px):
        for c in range(2):
            h, sig = token_pair(tok[2 * px + c], gain_ref[...], sigw_ref[...], cols, n_exp, width, up_at)
            hbuf[slot, c * rows:(c + 1) * rows, :] = h
            sigv_ref[pl.ds(pl.multiple_of((2 * px + c) * rows, rows), rows), :] = sig
        out = pltpu.make_async_copy(hbuf.at[slot], h_hbm.at[pl.ds(pl.multiple_of(2 * px * rows, 2 * rows), 2 * rows), :],
                                    out_sem.at[slot])
        p, a = pair_dots(hbuf[slot], cols, n_exp, width, up_at)
        prob[px] = p
        act_ref[:, pl.ds(pl.multiple_of(px * 2 * rows, 2 * rows), 2 * rows)] = a
        out.start()
        outs.append(out)

    def relay(arrived, block, row, vertical, forward=None):
        arrived.wait_recv()
        res = []
        if forward is not None:
            res.append(go(copy(block, row, piece, forward)))
        res.append(go(copy(block, row, piece, vertical)))
        res.append(go(copy(block, row, piece, to_mate)))
        return res

    lb, rb, fb = 2 * left + core, 2 * right + core, 2 * far + core
    f_r, v_l0, d1 = relay(s_r0, lb, m0, to_up, to_right)
    f_l, v_r1, d2 = relay(s_l1, rb, m1, to_down, to_left)
    s_mate.wait_recv()
    pair(0, x)
    v_l1, d3 = relay(s_r1, lb, m1, to_down)
    v_r0, d4 = relay(s_l0, rb, m0, to_up)
    o0 = half - mine
    o1 = o0 + piece

    def pass_on(arrived, block, row):
        arrived.wait_recv()
        return go(copy(block, row, piece, to_mate))

    e1 = pass_on(v_l0, lb, o0)
    e2 = pass_on(v_r1, rb, o1)
    v_f0, d5 = relay(f_r, fb, m0, to_up)
    v_f1, d6 = relay(f_l, fb, m1, to_down)
    e3 = pass_on(v_l1, lb, o1)
    e4 = pass_on(v_r0, rb, o0)
    for c in (d1, d3, e1, e3):
        c.wait_recv()
    pair(1, left)
    for c in (d2, d4, e2, e4):
        c.wait_recv()
    e5 = pass_on(v_f0, fb, o0)
    e6 = pass_on(v_f1, fb, o1)
    pair(2, right)
    for c in icopies:
        c.wait_recv()
    for c in (d5, d6, e5, e6):
        c.wait_recv()
    pair(3, far)

    first = pl.multiple_of(own * n_local, n_local)
    wt = jnp.concatenate([prob[b, pl.ds(first, n_local), :] for b in range(n_x)], axis=1)
    idx_t = jnp.concatenate([idx[b] for b in range(2 * n_x)], axis=1)
    routing_lists(idx_t, wt, first, n_local, lst_ref, wl_ref, cnt_ref)
    for c in started + icopies:
        c.wait_send()
    for c in outs:
        c.wait()


def run_gather(hidden, idx_t, gain, rw_t, sig_t, shg_t, shu_t, n_local, n_x):
    rows, dim = hidden.shape
    n_tok = rows * 2 * n_x
    n_hi = n_tok // LANES
    n_exp, width = rw_t.shape[0], shg_t.shape[0]
    pad = (width + 15) // 16 * 16
    n_copy = 5 + 2 * 3 + 2 * 2 + 2 * 2 + 6
    n_peer = 2 * n_x - 1
    vmem = pl.BlockSpec(memory_space=pltpu.VMEM)
    hbm = pl.BlockSpec(memory_space=pl.ANY)
    return pl.pallas_call(
        functools.partial(gather_kernel, n_local),
        out_shape=(jax.ShapeDtypeStruct((n_tok, dim), BF16),
                   jax.ShapeDtypeStruct((width, n_tok), BF16),
                   jax.ShapeDtypeStruct((n_tok, 1), F32),
                   jax.ShapeDtypeStruct((n_local * n_hi, LANES), jnp.int32),
                   jax.ShapeDtypeStruct((n_local * n_hi, LANES), F32),
                   jax.ShapeDtypeStruct((n_local, LANES), jnp.int32)),
        in_specs=[hbm, hbm] + [vmem] * 5,
        out_specs=[hbm] + [vmem] * 5,
        scratch_shapes=[
            pltpu.VMEM((2 * n_x, rows, dim), BF16),
            pltpu.VMEM((2 * n_x,) + idx_t.shape, jnp.int32),
            pltpu.VMEM((n_exp + 2 * pad, dim), BF16),
            pltpu.VMEM((n_x, n_exp, 2 * rows), F32),
            pltpu.VMEM((n_x, 2 * rows, dim), BF16),
            pltpu.SemaphoreType.DMA((2,)),
            pltpu.SemaphoreType.DMA((n_copy,)),
            pltpu.SemaphoreType.DMA((n_copy,)),
            pltpu.SemaphoreType.DMA((n_peer,)),
            pltpu.SemaphoreType.DMA((n_peer,)),
            pltpu.SemaphoreType.DMA((n_x,)),
        ],
        compiler_params=pltpu.CompilerParams(collective_id=0, has_side_effects=True, vmem_limit_bytes=32 * 1000 * 1000),
        name="gather",
    )(hidden, idx_t, gain, rw_t, sig_t, shg_t, shu_t)


def expert_kernel(lst, wl, cnt, h_hbm, act_ref, sig_ref, shd_ref, wg_hbm, wu_hbm, wd_hbm, out_hbm,
                  h_in, table, acc, wg, wu, wd, xt, xb, fb, ob, active, in_sem, w_sem, out_sem):
    n_tok, dim = h_hbm.shape
    n_local = wg_hbm.shape[0]
    n_chunk = dim // LANES
    n_blocks = n_tok // LANES

    def fetch_h(b):
        return pltpu.make_async_copy(h_hbm.at[pl.ds(b * LANES, LANES), :], h_in.at[b], in_sem.at[b])

    def weight_copies(e, s):
        return (pltpu.make_async_copy(wg_hbm.at[e], wg.at[s], w_sem.at[s, 0]),
                pltpu.make_async_copy(wu_hbm.at[e], wu.at[s], w_sem.at[s, 1]),
                pltpu.make_async_copy(wd_hbm.at[e], wd.at[s], w_sem.at[s, 2]))

    for b in range(n_blocks):
        fetch_h(b).start()

    def note(e, n):
        has = cnt[e, 0] > 0

        @pl.when(has)
        def _():
            active[n] = e

        return n + jnp.where(has, 1, 0)

    n_active = lax.fori_loop(0, n_local, note, 0)
    for s in range(SLOTS - 1):
        @pl.when(s < n_active)
        def _():
            for c in weight_copies(active[s], s):
                c.start()

    def clear(i, carry):
        acc[pl.ds(pl.multiple_of(i * 128, 128), 128), :] = jnp.zeros((128, LANES), F32)
        return carry

    lax.fori_loop(0, (n_tok * PITCH) // 128, clear, 0)
    acc[n_tok * PITCH:, :] = jnp.zeros((acc.shape[0] - n_tok * PITCH, LANES), F32)
    table[n_tok * PITCH:, :] = jnp.zeros((table.shape[0] - n_tok * PITCH, LANES), F32)

    def spread(b, carry):
        fetch_h(b).wait()
        for c in range(n_chunk):
            table[pl.ds(b * LANES * PITCH + c, LANES, stride=PITCH), :] = (
                h_in[b, :, c * LANES:(c + 1) * LANES].astype(F32))
        return carry

    lax.fori_loop(0, n_blocks, spread, 0)

    def list_at(e, r):
        return e * n_blocks + (r >> 7), r & (LANES - 1)

    def ffn(m, e, s, r0, n):
        stride = m + 8
        groups = (n + 7) // 8

        def gather(g, carry):
            hi, lo = list_at(e, r0 + g * 8)
            for i in range(8):
                r = g * 8 + i
                t = lst[hi, lo + i]
                slab = table[pl.ds(pl.multiple_of(t, 8), n_chunk), :]
                xt[pl.ds(r, n_chunk, stride=stride), :] = slab
            return carry

        lax.fori_loop(0, groups, gather, 0)
        for c in range(n_chunk):
            xb[:m, c * LANES:(c + 1) * LANES] = xt[c * stride:c * stride + m, :].astype(BF16)
        gate = lax.dot_general(wg[s], xb[:m, :], NT, preferred_element_type=F32)
        up = lax.dot_general(wu[s], xb[:m, :], NT, preferred_element_type=F32)
        act = (jax.nn.silu(gate) * up).astype(BF16)
        for c in range(0, n_chunk, 2):
            f = lax.dot_general(act, wd[s, :, c * LANES:(c + 2) * LANES], TN, preferred_element_type=F32)
            fb[c * stride:c * stride + m, :] = f[:, :LANES]
            fb[(c + 1) * stride:(c + 1) * stride + m, :] = f[:, LANES:]

        def scatter(g, carry):
            where, old, new = [], [], []
            hi, lo = list_at(e, r0 + g * 8)
            for i in range(8):
                t = lst[hi, lo + i]
                where.append(pl.multiple_of(t, 8))
                old.append(acc[pl.ds(where[i], n_chunk), :])
            for i in range(8):
                r = g * 8 + i
                w = wl[hi, lo + i]
                new.append(old[i] + w * fb[pl.ds(r, n_chunk, stride=stride), :])
            for i in range(8):
                acc[pl.ds(where[i], n_chunk), :] = new[i]
            return carry

        lax.fori_loop(0, groups, scatter, 0)

    big = TILES[-1]

    def expert(i, carry):
        e = active[i]
        s = lax.rem(i, SLOTS)
        ahead = i + SLOTS - 1

        @pl.when(ahead < n_active)
        def _():
            for c in weight_copies(active[ahead], lax.rem(ahead, SLOTS)):
                c.start()

        for c in weight_copies(e, s):
            c.wait()
        total = cnt[e, 0]

        def piece(j, carry2):
            r0 = j * big
            n = jnp.minimum(total - r0, big)
            below = 0
            for m in TILES:
                @pl.when((n > below) & (n <= m))
                def _(m=m):
                    ffn(m, e, s, r0, n)
                below = m
            return carry2

        lax.fori_loop(0, (total + big - 1) // big, piece, 0)
        return carry

    lax.fori_loop(0, n_active, expert, 0)

    def write_out(b, slot):
        return pltpu.make_async_copy(ob.at[slot], out_hbm.at[pl.ds(b * LANES, LANES), :], out_sem.at[slot])

    def finish(b, carry):
        slot = lax.rem(b, 2)

        @pl.when(b >= 2)
        def _():
            write_out(b - 2, slot).wait()

        rows = pl.ds(pl.multiple_of(b * LANES, LANES), LANES)
        sig = sig_ref[rows, :]
        for c in range(0, n_chunk, 2):
            sh = sig * lax.dot_general(act_ref[:, rows], shd_ref[:, c * LANES:(c + 2) * LANES], TN,
                                       preferred_element_type=F32)
            for d in range(2):
                routed = acc[pl.ds(b * LANES * PITCH + c + d, LANES, stride=PITCH), :]
                ob[slot, :, (c + d) * LANES:(c + d + 1) * LANES] = (
                    routed + sh[:, d * LANES:(d + 1) * LANES]).astype(BF16)
        write_out(b, slot).start()
        return carry

    lax.fori_loop(0, n_blocks, finish, 0)
    for b in (n_blocks - 2, n_blocks - 1):
        write_out(b, b % 2).wait()


def run_experts(lst, wl, cnt, h, act, sig, shd, wg, wu, wd):
    n_tok, dim = h.shape
    n_local, width, _ = wg.shape
    n_chunk = dim // LANES
    big = TILES[-1]
    smem = pl.BlockSpec(memory_space=pltpu.SMEM)
    vmem = pl.BlockSpec(memory_space=pltpu.VMEM)
    hbm = pl.BlockSpec(memory_space=pl.ANY)
    return pl.pallas_call(
        expert_kernel,
        out_shape=jax.ShapeDtypeStruct((n_tok, dim), BF16),
        in_specs=[smem] * 3 + [hbm] + [vmem] * 3 + [hbm] * 3,
        out_specs=hbm,
        scratch_shapes=[
            pltpu.VMEM((n_tok // LANES, LANES, dim), BF16),
            pltpu.VMEM(((n_tok + 1) * PITCH, LANES), F32),
            pltpu.VMEM(((n_tok + 1) * PITCH, LANES), F32),
            pltpu.VMEM((SLOTS, width, dim), BF16),
            pltpu.VMEM((SLOTS, width, dim), BF16),
            pltpu.VMEM((SLOTS, width, dim), BF16),
            pltpu.VMEM((n_chunk * (big + 8), LANES), F32),
            pltpu.VMEM((big, dim), BF16),
            pltpu.VMEM((n_chunk * (big + 8), LANES), F32),
            pltpu.VMEM((2, LANES, dim), BF16),
            pltpu.SMEM((n_local,), jnp.int32),
            pltpu.SemaphoreType.DMA((n_tok // LANES,)),
            pltpu.SemaphoreType.DMA((SLOTS, 3)),
            pltpu.SemaphoreType.DMA((2,)),
        ],
        compiler_params=pltpu.CompilerParams(vmem_limit_bytes=64 * 1000 * 1000),
        name="experts",
    )(lst, wl, cnt, h, act, sig, shd, wg, wu, wd)


def reduce_kernel(groups, p_hbm, x_ref, out_ref, mate, own, ra, rb, rc, s_in, s_d, r_d, s_a, r_a, s_b, r_b, s_c, r_c,
                  s_e, r_e):
    x, core, y, n_x, n_y = place()
    rows, dim = x_ref.shape
    wide = dim // len(groups)
    part = rows // n_y

    def at(v, n):
        return lax.rem(v + n, n)

    xs = [at(x + d, n_x) for d in range(4)]
    ys = [at(y + d, n_y) for d in range(4)]
    to_mate = peer(x, 1 - core, y)
    x_peers = [None] + [peer(xs[d], core, y) for d in range(1, 4)]
    y_peers = [None] + [peer(x, core, ys[d]) for d in range(1, 4)]

    loads, mates = [], []
    for g in range(len(groups)):
        c = pltpu.make_async_copy(p_hbm.at[:, core, :, g * wide:(g + 1) * wide], own.at[g], s_in.at[g])
        c.start()
        loads.append(c)
    meet([to_mate] + x_peers[1:] + y_peers[1:])
    started = []

    def go(c):
        c.start()
        started.append(c)
        return c

    for g in range(len(groups)):
        mates.append(go(remote(p_hbm.at[:, 1 - core, :, g * wide:(g + 1) * wide], mate.at[g], s_d.at[g], r_d.at[g],
                               to_mate)))

    def unit(g, d, lo, n):
        if groups[g] == "x":
            return own.at[g, xs[d], lo:lo + n, :]
        return own.at[g, :, pl.ds(pl.multiple_of(ys[d] * part, part) + lo, n), :]

    a, b_ind, b_dep = {}, {}, {}
    for g, kind in enumerate(groups):
        loads[g].wait()
        mates[g].wait_recv()
        own[g] = (own[g].astype(F32) + mate[g].astype(F32)).astype(BF16)
        peers = x_peers if kind == "x" else y_peers
        full = rows if kind == "x" else part
        h = full // 2
        land = (lambda r: r) if kind == "x" else (lambda r: r)
        for k, (lo, d) in enumerate(((0, 1), (h, 3))):
            a[g, k] = go(remote(unit(g, 2, lo, h), ra[kind].at[groups[:g].count(kind), k], s_a.at[g, k], r_a.at[g, k],
                                peers[d]))
        for k, (lo, d) in enumerate(((h, 1), (0, 3))):
            dst = rb[kind].at[groups[:g].count(kind), k]
            dst = dst.at[lo:lo + h, :] if kind == "x" else dst.at[:, lo:lo + h, :]
            b_ind[g, k] = go(remote(unit(g, d, lo, h), dst, s_b.at[g, k, 0], r_b.at[g, k, 0], peers[d]))
    for g, kind in enumerate(groups):
        peers = x_peers if kind == "x" else y_peers
        full = rows if kind == "x" else part
        h = full // 2
        n = groups[:g].count(kind)
        for k, (lo, d) in enumerate(((0, 1), (h, 3))):
            a[g, k].wait_recv()
            ref = unit(g, d, lo, h)
            ref[...] = (ref[...].astype(F32) + ra[kind][n, k].astype(F32)).astype(BF16)
        for k, (lo, d) in enumerate(((0, 1), (h, 3))):
            dst = rb[kind].at[n, k]
            dst = dst.at[lo:lo + h, :] if kind == "x" else dst.at[:, lo:lo + h, :]
            b_dep[g, k] = go(remote(unit(g, d, lo, h), dst, s_b.at[g, k, 1], r_b.at[g, k, 1], peers[d]))
    c_sent = {}
    for g, kind in enumerate(groups):
        n = groups[:g].count(kind)
        for k in range(2):
            b_ind[g, k].wait_recv()
            b_dep[g, k].wait_recv()
        full = rows if kind == "x" else part
        ref = unit(g, 0, 0, full)
        ref[...] = (ref[...].astype(F32) + rb[kind][n, 0].astype(F32) + rb[kind][n, 1].astype(F32)).astype(BF16)
        for d in range(1, 4):
            if kind == "x":
                src = own.at[g, x, pl.ds(pl.multiple_of(ys[d] * part, part), part), :]
                where = y_peers[d]
            else:
                src = own.at[g, xs[d], pl.ds(pl.multiple_of(y * part, part), part), :]
                where = x_peers[d]
            c_sent[g, d] = go(remote(src, rc.at[g, d - 1], s_c.at[g, d - 1], r_c.at[g, d - 1], where))
    e_sent = {}
    mine = pl.ds(pl.multiple_of(y * part, part), part)
    for g, kind in enumerate(groups):
        cols = slice(g * wide, (g + 1) * wide)
        total = own[g, x, mine, :].astype(F32)
        for d in range(1, 4):
            c_sent[g, d].wait_recv()
            total = total + rc[g, d - 1].astype(F32)
        out_ref[mine, cols] = (x_ref[mine, cols].astype(F32) + total).astype(BF16)
        for d in range(1, 4):
            ref = out_ref.at[mine, cols]
            e_sent[g, d] = go(remote(ref, ref, s_e.at[g, d - 1], r_e.at[g, d - 1], y_peers[d]))
    for g in range(len(groups)):
        for d in range(1, 4):
            e_sent[g, d].wait_recv()
    for c in started:
        c.wait_send()


def run_reduce(partial, hidden, n_x, n_y):
    rows, dim = hidden.shape
    groups = ("y", "x", "x", "x")
    n_g = len(groups)
    wide = dim // n_g
    part = rows // n_y
    dma = pltpu.SemaphoreType.DMA
    n_kind = {k: groups.count(k) for k in ("x", "y")}

    def kernel(p, xr, o, mate, own, ra_x, ra_y, rb_x, rb_y, *rest):
        reduce_kernel(groups, p, xr, o, mate, own, {"x": ra_x, "y": ra_y}, {"x": rb_x, "y": rb_y}, *rest)

    return pl.pallas_call(
        kernel,
        out_shape=jax.ShapeDtypeStruct((rows, dim), BF16),
        in_specs=[pl.BlockSpec(memory_space=pl.ANY), pl.BlockSpec(memory_space=pltpu.VMEM)],
        out_specs=pl.BlockSpec(memory_space=pltpu.VMEM),
        scratch_shapes=[
            pltpu.VMEM((n_g, n_x, rows, wide), BF16),
            pltpu.VMEM((n_g, n_x, rows, wide), BF16),
            pltpu.VMEM((n_kind["x"], 2, rows // 2, wide), BF16),
            pltpu.VMEM((n_kind["y"], 2, n_x, part // 2, wide), BF16),
            pltpu.VMEM((n_kind["x"], 2, rows, wide), BF16),
            pltpu.VMEM((n_kind["y"], 2, n_x, part, wide), BF16),
            pltpu.VMEM((n_g, 3, part, wide), BF16),
            dma((n_g,)), dma((n_g,)), dma((n_g,)),
            dma((n_g, 2)), dma((n_g, 2)),
            dma((n_g, 2, 2)), dma((n_g, 2, 2)),
            dma((n_g, 3)), dma((n_g, 3)),
            dma((n_g, 3)), dma((n_g, 3)),
        ],
        compiler_params=pltpu.CompilerParams(collective_id=1, has_side_effects=True, vmem_limit_bytes=32 * 1000 * 1000),
        name="reduce",
    )(partial.reshape(n_x, 2, rows, dim), hidden)


def solution(mesh):
    tok_spec = P(('dp', 'ep'), None)
    in_specs = (tok_spec, tok_spec, P(None), P(None, None), P(None, None),
                P('ep', None, 'tp'), P('ep', None, 'tp'), P('ep', 'tp', None),
                P(None, ('tp', 'ep')), P(None, ('tp', 'ep')), P(('tp', 'ep'), None))
    n_x, n_y = mesh.shape['ep'] // 2, mesh.shape['tp']
    assert n_x == 4 and n_y == 4

    def local_step(hidden_in, topk_idx, norm_gain, router_w, shared_sig_w, exp_gate, exp_up, exp_down,
                   sh_gate, sh_up, sh_down):
        h, act, sig, lst, wl, cnt = run_gather(
            hidden_in, topk_idx.T, norm_gain.reshape(1, -1), router_w.T, shared_sig_w.T, sh_gate.T, sh_up.T,
            exp_gate.shape[0], n_x)
        partial = run_experts(lst, wl, cnt, h, act, sig, sh_down,
                              jnp.swapaxes(exp_gate, 1, 2), jnp.swapaxes(exp_up, 1, 2), exp_down)
        return run_reduce(partial, hidden_in, n_x, n_y)

    return jax.shard_map(local_step, mesh=mesh, in_specs=in_specs, out_specs=tok_spec, check_vma=False)
```

time: 212 us -> 105 us (0.50)
  waiting for transfers between devices: 103 us -> 0 us
  Pallas kernels: 35.1 us -> 89.6 us
  local copies, waits for them, and re-layouts: 40 us -> 14.2 us
  blocking collectives: 19 us -> 0 us
  between operations: 13.1 us -> 0.06 us
    reduce_scatter x1 -> x0, waiting for transfers between devices: 61.9 us -> none  [local_step(): own_rows = lax.psum_scatter(partial, 'ep', scatter_dimension=0, tiled=True)]
    pallas_call x1 -> x2, Pallas kernels: 11.8 us -> 54.8 us  [the longest x1 28.3 us: run_gather(): pl.pallas_call(functools.partial(gather_kernel, n_local), out_shape=(jax....]
    psum x1 -> x0, waiting for transfers between devices: 39.8 us -> none  [local_step(): total = lax.psum(own_rows, 'tp')]
    unnamed x10 -> x29, local copies, waits for them, and re-layouts: 38.7 us -> 13.5 us
    all_gather x1 -> x0, blocking collectives: 19 us -> none  [local_step(): all_idx = lax.all_gather(idx_t, 'ep', axis=1, tiled=True)]
    pallas_call x1, Pallas kernels: 23.3 us -> 34.8 us  [run_experts(): pl.pallas_call(expert_kernel, out_shape=jax.ShapeDtypeStruct((n_tok, dim)...]
  transfers between devices with their start and end apart: 3 -> 0, of which waited for: 2 -> 0; matrix products, arithmetic and copies ran while one was open for 19% -> 0% of each run, Pallas kernels for 0% -> 0%
where the time goes in v2:
time: 105 us; the launch traced here: 104 us
  Pallas kernels  89.6 us (85%)
  local copies, waits for them, and re-layouts  14.2 us (14%)
    pallas_call x1, Pallas kernels, run_experts(): pl.pallas_call(expert_kernel, out_shape=jax.ShapeDtypeStruct((n_tok, dim)...  34.8 us
    pallas_call x1, Pallas kernels, run_gather(): pl.pallas_call(functools.partial(gather_kernel, n_local), out_shape=(jax....  28.3 us
    pallas_call x1, Pallas kernels, run_reduce(): pl.pallas_call(kernel, out_shape=jax.ShapeDtypeStruct((rows, dim), BF16),...  26.5 us
    unnamed x29, local copies, waits for them, and re-layouts  13.5 us

profile of v2, /device:TPU:97, one launch (start us, length us, event | category | flops | bytes accessed | tf_op | source)
XLA Modules:
  0.0 103.9 jit_solution(11489810974092588979)
XLA Ops:
  0.0 0.7 reshape.6.gain_ref
  0.7 0.0 copy-start.2
  0.7 1.0 %copy-done.2 = bf16[128,2048]{1,0:T(8,128)(2,1)S(1)} copy-done((bf16[128,2048]{1,0:T(8,128)(2,1)S(1)}, bf16[128,2048]{1,0:T(8,128)(2,1)}, u32[]{:S(2)}) %copy-start.2) | copy-done | bytes 524312
  1.7 0.0 copy-start.5
  1.7 1.0 copy-done.5
  2.7 0.0 copy-start.6
  2.7 1.0 copy-done.6
  3.7 0.0 copy-start.7
  3.7 0.9 copy-done.7
  4.7 0.0 copy-start.11
  4.7 0.7 copy-done.11
  5.4 0.0 copy-start.12
  5.4 0.7 copy-done.12
  6.0 28.3 %gather.1 = (bf16[1024,2048]{1,0:T(8,128)(2,1)S(1)}, bf16[88,1024]{1,0:T(8,128)(2,1)S(1)}, f32[1024,1]{1,0:T(8,128)S(1)}, s32[64,128]{1,0:T(8,128)S(1)}, f32[64,128]{1,0:T(8,128)S(1)}, /*index=5*/s32[8,128]{1,0:T(8,128)S(1)}) custom-call(bf16[128,2048]{1,0:T(8,128)(2,1)S(1)} %copy-done.2, s32[6,128]{1,0:T(8,128)S(1)} %bitcast.13, ...), custom_call_target="tpu_custom_call" | custom-call | tf_op jit(solution)/shard_map/gather/pallas_call | solution.py:244
  34.4 0.0 copy-start.1
  34.4 1.9 %copy-done.1 = bf16[1024,2048]{1,0:T(8,128)(2,1)} copy-done((bf16[1024,2048]{1,0:T(8,128)(2,1)}, bf16[1024,2048]{1,0:T(8,128)(2,1)S(1)}, u32[]{:S(2)}) %copy-start.1) | copy-done | bytes 4194328
  36.3 0.0 copy-start.4
  36.3 0.8 copy-done.4
  37.1 0.0 copy-start.8
  37.1 0.7 copy-done.8
  37.8 0.0 copy-start.9
  37.8 0.6 copy-done.9
  38.4 0.0 copy-start.10
  38.4 0.6 copy-done.10
  39.0 0.0 copy-start.13
  39.0 0.6 copy-done.13
  39.6 0.0 copy-start.3
  39.6 34.8 %experts.1 = bf16[1024,2048]{1,0:T(8,128)(2,1)} custom-call(s32[64,128]{1,0:T(8,128)} %copy-done.9, f32[64,128]{1,0:T(8,128)} %copy-done.10, s32[8,128]{1,0:T(8,128)} %copy-done.13, bf16[1024,2048]{1,0:T(8,128)(2,1)} %copy-done.1, bf16[88,1024]{1,0:T(8,128)(2,1)} %copy-done.8, f32[1024,1]{1,0:T(8,128)} %copy-done.4, bf16[88,2048]{1,0:T(8,128)(2,1)} %shd_ref.1, ...), custom_call_target="tpu_custom_call" | custom-call | tf_op jit(solution)/shard_map/experts/pallas_call | solution.py:434
  74.4 0.0 copy-done.3
  74.4 0.0 copy-start
  74.4 2.2 %copy-done = bf16[1024,2048]{1,0:T(8,128)(2,1)S(1)} copy-done((bf16[1024,2048]{1,0:T(8,128)(2,1)S(1)}, bf16[1024,2048]{1,0:T(8,128)(2,1)}, u32[]{:S(2)}) %copy-start) | copy-done | bytes 4194328
  76.6 26.5 %reduce.1 = bf16[128,2048]{1,0:T(8,128)(2,1)S(1)} custom-call(bf16[4,2,128,2048]{3,2,1,0:T(8,128)(2,1)S(1)} %bitcast.8, bf16[128,2048]{1,0:T(8,128)(2,1)S(1)} %copy-done.3), custom_call_target="tpu_custom_call" | custom-call | tf_op jit(solution)/shard_map/reduce/pallas_call | solution.py:575
  103.1 0.8 copy.13
Async XLA Ops:
  0.7 1.0 %copy-start.2 = (bf16[128,2048]{1,0:T(8,128)(2,1)S(1)}, bf16[128,2048]{1,0:T(8,128)(2,1)}, u32[]{:S(2)}) copy-start(bf16[128,2048]{1,0:T(8,128)(2,1)} %xr.1) | copy-start | bytes 1572868
  1.7 1.0 copy-start.5
  2.7 1.0 copy-start.6
  3.7 0.9 copy-start.7
  4.7 0.7 copy-start.11
  5.4 0.7 copy-start.12
  34.4 1.9 %copy-start.1 = (bf16[1024,2048]{1,0:T(8,128)(2,1)}, bf16[1024,2048]{1,0:T(8,128)(2,1)S(1)}, u32[]{:S(2)}) copy-start(bf16[1024,2048]{1,0:T(8,128)(2,1)S(1)} %get-tuple-element.14.h_hbm) | copy-start | bytes 12582916
  36.3 0.8 copy-start.4
  37.1 0.7 copy-start.8
  37.8 0.6 copy-start.9
  38.4 0.6 copy-start.10
  39.0 0.6 copy-start.13
  39.6 34.8 %copy-start.3 = (bf16[128,2048]{1,0:T(8,128)(2,1)S(1)}, bf16[128,2048]{1,0:T(8,128)(2,1)}, u32[]{:S(2)}) copy-start(bf16[128,2048]{1,0:T(8,128)(2,1)} %xr.1) | copy-start | bytes 1572868
  74.4 2.2 %copy-start = (bf16[1024,2048]{1,0:T(8,128)(2,1)S(1)}, bf16[1024,2048]{1,0:T(8,128)(2,1)}, u32[]{:S(2)}) copy-start(bf16[1024,2048]{1,0:T(8,128)(2,1)} %experts.1) | copy-start | bytes 12582916

commit v3 on v2

--- a/solution.py
+++ b/solution.py
@@ -264,7 +264,7 @@
             pltpu.SemaphoreType.DMA((n_peer,)),
             pltpu.SemaphoreType.DMA((n_x,)),
         ],
-        compiler_params=pltpu.CompilerParams(collective_id=0, has_side_effects=True, vmem_limit_bytes=32 * 1000 * 1000),
+        compiler_params=pltpu.CompilerParams(collective_id=0, has_side_effects=True, vmem_limit_bytes=67_000_000),
         name="gather",
     )(hidden, idx_t, gain, rw_t, sig_t, shg_t, shu_t)
 
@@ -452,7 +452,7 @@
             pltpu.SemaphoreType.DMA((SLOTS, 3)),
             pltpu.SemaphoreType.DMA((2,)),
         ],
-        compiler_params=pltpu.CompilerParams(vmem_limit_bytes=64 * 1000 * 1000),
+        compiler_params=pltpu.CompilerParams(vmem_limit_bytes=67_000_000),
         name="experts",
     )(lst, wl, cnt, h, act, sig, shd, wg, wu, wd)
 
@@ -591,7 +591,7 @@
             dma((n_g, 3)), dma((n_g, 3)),
             dma((n_g, 3)), dma((n_g, 3)),
         ],
-        compiler_params=pltpu.CompilerParams(collective_id=1, has_side_effects=True, vmem_limit_bytes=32 * 1000 * 1000),
+        compiler_params=pltpu.CompilerParams(collective_id=1, has_side_effects=True, vmem_limit_bytes=67_000_000),
         name="reduce",
     )(partial.reshape(n_x, 2, rows, dim), hidden)
 

time: 105 us -> 96.2 us (0.916)
  local copies, waits for them, and re-layouts: 14.2 us -> 3.17 us
  Pallas kernels: 89.6 us -> 91.1 us
    unnamed x29 -> x1, local copies, waits for them, and re-layouts: 13.5 us -> 1.88 us
    pallas_call x1, Pallas kernels: 34.8 us -> 28.8 us  [run_experts(): pl.pallas_call(expert_kernel, out_shape=jax.ShapeDtypeStruct((n_tok, dim)...]
    pallas_call x1, Pallas kernels: 26.5 us -> 32.2 us  [run_reduce(): pl.pallas_call(kernel, out_shape=jax.ShapeDtypeStruct((rows, dim), BF16),...]
    pallas_call x1, Pallas kernels: 28.3 us -> 30.1 us  [run_gather(): pl.pallas_call(functools.partial(gather_kernel, n_local), out_shape=(jax....]
where the time goes in v3:
time: 96.2 us; the launch traced here: 94.3 us
  Pallas kernels  91.1 us (95%)
  local copies, waits for them, and re-layouts  3.17 us (3%)
    pallas_call x1, Pallas kernels, run_reduce(): pl.pallas_call(kernel, out_shape=jax.ShapeDtypeStruct((rows, dim), BF16),...  32.2 us
    pallas_call x1, Pallas kernels, run_gather(): pl.pallas_call(functools.partial(gather_kernel, n_local), out_shape=(jax....  30.1 us
    pallas_call x1, Pallas kernels, run_experts(): pl.pallas_call(expert_kernel, out_shape=jax.ShapeDtypeStruct((n_tok, dim)...  28.8 us

profile of v3, /device:TPU:97, one launch (start us, length us, event | category | flops | bytes accessed | tf_op | source)
XLA Modules:
  0.0 94.3 jit_solution(11005454392882875084)
XLA Ops:
  0.0 1.3 %reshape.6.gain_ref = bf16[1,2048]{1,0:T(2,128)(2,1)} reshape(bf16[2048]{0:T(1024)(128)(2,1)} %param.13) | data formatting | bytes 8192 | tf_op jit(solution)/shard_map/reshape | solution.py:610
  1.3 30.1 %gather.1 = (bf16[1024,2048]{1,0:T(8,128)(2,1)}, bf16[88,1024]{1,0:T(8,128)(2,1)}, f32[1024,1]{1,0:T(8,128)}, s32[64,128]{1,0:T(8,128)}, f32[64,128]{1,0:T(8,128)}, /*index=5*/s32[8,128]{1,0:T(8,128)}) custom-call(bf16[128,2048]{1,0:T(8,128)(2,1)} %xr.1, s32[6,128]{1,0:T(8,128)} %bitcast.15, bf16[1,2048]{1,0:T(2,128)(2,1)} %reshape.6.gain_ref, ...), custom_call_target="tpu_custom_call" | custom-call | tf_op jit(solution)/shard_map/gather/pallas_call | solution.py:244
  31.4 28.8 %experts.1 = bf16[1024,2048]{1,0:T(8,128)(2,1)} custom-call(s32[64,128]{1,0:T(8,128)} %get-tuple-element.11.lst, f32[64,128]{1,0:T(8,128)} %get-tuple-element.12.wl, s32[8,128]{1,0:T(8,128)} %get-tuple-element.13.cnt, bf16[1024,2048]{1,0:T(8,128)(2,1)} %get-tuple-element.14.h_hbm, bf16[88,1024]{1,0:T(8,128)(2,1)} %get-tuple-element.15.act_ref, ...), custom_call_target="tpu_custom_call" | custom-call | tf_op jit(solution)/shard_map/experts/pallas_call | solution.py:434
  60.2 32.2 %reduce.1 = bf16[128,2048]{1,0:T(8,128)(2,1)} custom-call(bf16[4,2,128,2048]{3,2,1,0:T(8,128)(2,1)} %bitcast.8, bf16[128,2048]{1,0:T(8,128)(2,1)} %xr.1), custom_call_target="tpu_custom_call" | custom-call | tf_op jit(solution)/shard_map/reduce/pallas_call | solution.py:575
  92.5 1.9 %copy.13 = bf16[128,2048]{1,0:T(8,128)(2,1)} copy(bf16[128,2048]{1,0:T(8,128)(2,1)} %reduce.1) | data formatting | bytes 1048576

commit v4 on v3

v4 whole, which is shorter than its diff:
```python
import functools

import jax
import jax.numpy as jnp
from jax import lax
from jax.experimental import pallas as pl
from jax.experimental.pallas import tpu as pltpu
from jax.sharding import PartitionSpec as P

RMS_EPS = 1e-6
LANES = 128
PITCH = 20
PAD = 4
TILES = (64, 256, 320, 384, 512)
SLOTS = 3
F32 = jnp.float32
BF16 = jnp.bfloat16
NT = (((1,), (1,)), ((), ()))
TN = (((0,), (0,)), ((), ()))
MESH = pl.DeviceIdType.MESH


def place():
    ep, y = lax.axis_index("ep"), lax.axis_index("tp")
    return ep // 2, ep % 2, y, lax.axis_size("ep") // 2, lax.axis_size("tp")


def peer(x, core, y):
    return {"ep": 2 * x + core, "tp": y}


def remote(src, dst, send, recv, where):
    return pltpu.make_async_remote_copy(src_ref=src, dst_ref=dst, send_sem=send, recv_sem=recv,
                                        device_id=where, device_id_type=MESH)


def meet(peers):
    barrier = pltpu.get_barrier_semaphore()
    for p in peers:
        pl.semaphore_signal(barrier, inc=1, device_id=p, device_id_type=MESH)
    pl.semaphore_wait(barrier, len(peers))


def token_pair(x, gain, sigw, cols_ref, n_exp, width, up_at):
    xf = x.astype(F32)
    inv = lax.rsqrt(jnp.mean(xf * xf, axis=-1, keepdims=True) + RMS_EPS)
    h = (xf * inv * gain.astype(F32)).astype(BF16)
    sig = jax.nn.sigmoid(jnp.sum(h.astype(F32) * sigw.astype(F32), axis=-1, keepdims=True))
    return h, sig


def pair_dots(h, cols_ref, n_exp, width, up_at):
    out = lax.dot_general(cols_ref[...], h, NT, preferred_element_type=F32)
    logits = out[:n_exp]
    ex = jnp.exp(logits - jnp.max(logits, axis=0, keepdims=True))
    prob = ex / jnp.sum(ex, axis=0, keepdims=True)
    act = (jax.nn.silu(out[n_exp:n_exp + width]) * out[up_at:up_at + width]).astype(BF16)
    return prob, act


def routing_lists(idx_t, first, n_local, lst_ref, cnt_ref):
    n_tok = idx_t.shape[1]
    n_hi = n_tok // LANES
    sub = lax.broadcasted_iota(jnp.int32, (n_local, n_tok), 0)
    member = jnp.zeros((n_local, n_tok), F32)
    for e in range(n_local):
        hit = jnp.sum((idx_t == first + e).astype(F32), axis=0, keepdims=True)
        member = jnp.where(sub == e, hit, member)
    tri = (lax.broadcasted_iota(jnp.int32, (LANES, LANES), 0)
           < lax.broadcasted_iota(jnp.int32, (LANES, LANES), 1)).astype(F32).astype(BF16)
    base = jnp.zeros((n_local, 1), F32)
    parts = []
    for b in range(n_hi):
        m_b = member[:, b * LANES:(b + 1) * LANES]
        parts.append(jnp.dot(m_b.astype(BF16), tri, preferred_element_type=F32) + base)
        base = base + jnp.sum(m_b, axis=-1, keepdims=True)
    pos = jnp.concatenate(parts, axis=1).astype(jnp.int32)
    cnt_ref[...] = jnp.broadcast_to(base, cnt_ref.shape).astype(jnp.int32)
    tok = lax.broadcasted_iota(jnp.int32, (n_hi, n_tok), 1)
    hi_id = lax.broadcasted_iota(jnp.int32, (n_hi, n_tok), 0)
    lo_id = lax.broadcasted_iota(jnp.int32, (LANES, n_tok), 0)
    row_id = (lax.broadcasted_iota(jnp.int32, (n_hi, LANES), 0) * LANES
              + lax.broadcasted_iota(jnp.int32, (n_hi, LANES), 1))
    tok_hi = (tok >> 3).astype(F32)
    tok_lo = (tok & 7).astype(F32)
    for e in range(n_local):
        p_e = pos[e:e + 1, :]
        here = ((p_e >> 7) == hi_id) & (member[e:e + 1, :] > 0.0)
        lo_hot = jnp.where((p_e & (LANES - 1)) == lo_id, 1.0, 0.0).astype(BF16)
        lhs = jnp.concatenate([jnp.where(here, v, 0.0) for v in (tok_hi, tok_lo)], axis=0).astype(BF16)
        got = lax.dot_general(lhs, lo_hot, NT, preferred_element_type=F32)
        t_of = (got[:n_hi] * 8.0 + got[n_hi:]).astype(jnp.int32)
        valid = row_id < base[e:e + 1, :].astype(jnp.int32)
        lst_ref[e * n_hi:(e + 1) * n_hi, :] = jnp.where(valid, t_of, n_tok)


def gather_kernel(n_local, x_hbm, idx_hbm, gain_ref, rw_ref, sigw_ref, shg_ref, shu_ref,
                  h_hbm, act_ref, sigv_ref, lst_ref, wl_ref, cnt_ref,
                  tok, idx, cols, prob, hbuf, in_sem, send, recv, isend, irecv, out_sem):
    x, core, y, n_x, n_y = place()
    n_exp, width = rw_ref.shape[0], shg_ref.shape[0]
    up_at = n_exp + (width + 15) // 16 * 16
    rows = x_hbm.shape[0]
    half, piece = rows // 2, rows // 8
    own = 2 * x + core
    load_x = pltpu.make_async_copy(x_hbm, tok.at[own], in_sem.at[0])
    load_i = pltpu.make_async_copy(idx_hbm, idx.at[own], in_sem.at[1])
    load_x.start()
    load_i.start()

    def at(v, n):
        return lax.rem(v + n, n)

    right, left, far = at(x + 1, n_x), at(x - 1, n_x), at(x + 2, n_x)
    up, down = at(y + 1, n_y), at(y - 1, n_y)
    others = [peer(x, 1 - core, y)]
    for d in (right, left, far):
        for c in (core, 1 - core):
            others.append(peer(d, c, y))
    meet(others + [peer(x, core, up), peer(x, core, down)])
    load_x.wait()
    load_i.wait()

    started = []
    count = [0]

    def copy(block, row, n_rows, where):
        k = count[0]
        count[0] += 1
        row = pl.multiple_of(row, piece)
        ref = tok.at[block, pl.ds(row, n_rows), :]
        c = remote(ref, ref, send.at[k], recv.at[k], where)
        return c

    def go(c):
        c.start()
        started.append(c)
        return c

    mine = (y % 2) * half
    m = [mine + k * piece for k in range(4)]
    o = [half - mine + k * piece for k in range(4)]
    to_right, to_left = peer(right, core, y), peer(left, core, y)
    to_up, to_down, to_mate = peer(x, core, up), peer(x, core, down), peer(x, 1 - core, y)
    from_left, from_right = {}, {}
    for k in range(4):
        from_left[k] = go(copy(own, m[k], piece, to_right))
        from_right[k ^ 2] = go(copy(own, m[k ^ 2], piece, to_left))
    s_mate = go(copy(own, 0, rows, to_mate))
    icopies = []
    for k, p in enumerate(others):
        c = remote(idx.at[own], idx.at[own], isend.at[k], irecv.at[k], p)
        c.start()
        icopies.append(c)

    cols[...] = jnp.zeros_like(cols)
    cols[:n_exp, :] = rw_ref[...]
    cols[n_exp:n_exp + width, :] = shg_ref[...]
    cols[up_at:up_at + width, :] = shu_ref[...]

    outs = []

    def pair(slot, px):
        for c in range(2):
            h, sig = token_pair(tok[2 * px + c], gain_ref[...], sigw_ref[...], cols, n_exp, width, up_at)
            hbuf[slot, c * rows:(c + 1) * rows, :] = h
            sigv_ref[pl.ds(pl.multiple_of((2 * px + c) * rows, rows), rows), :] = sig
        out = pltpu.make_async_copy(hbuf.at[slot], h_hbm.at[pl.ds(pl.multiple_of(2 * px * rows, 2 * rows), 2 * rows), :],
                                    out_sem.at[slot])
        p, a = pair_dots(hbuf[slot], cols, n_exp, width, up_at)
        prob[px] = p
        act_ref[:, pl.ds(pl.multiple_of(px * 2 * rows, 2 * rows), 2 * rows)] = a
        out.start()
        outs.append(out)

    lb, rb, fb = 2 * left + core, 2 * right + core, 2 * far + core
    mate = {lb_name: [] for lb_name in "lrf"}
    along_y, forward = {}, {}

    def relay(name, block, k, arrived, onward=None):
        arrived.wait_recv()
        if onward is not None:
            forward[k] = go(copy(block, m[k], piece, onward))
        along_y[name, k] = go(copy(block, m[k], piece, to_up if k < 2 else to_down))
        mate[name].append(go(copy(block, m[k], piece, to_mate)))

    def pass_on(name, block, k):
        along_y[name, k].wait_recv()
        mate[name].append(go(copy(block, o[k], piece, to_mate)))

    def arrived_all(name):
        for c in mate[name]:
            c.wait_recv()

    relay("l", lb, 0, from_left[0], to_right)
    relay("r", rb, 2, from_right[2], to_left)
    relay("l", lb, 1, from_left[1], to_right)
    relay("r", rb, 3, from_right[3], to_left)
    s_mate.wait_recv()
    pair(0, x)
    relay("l", lb, 2, from_left[2])
    relay("r", rb, 0, from_right[0])
    pass_on("l", lb, 0)
    pass_on("r", rb, 2)
    relay("l", lb, 3, from_left[3])
    relay("r", rb, 1, from_right[1])
    pass_on("l", lb, 1)
    pass_on("r", rb, 3)
    relay("f", fb, 0, forward[0])
    relay("f", fb, 2, forward[2])
    pass_on("l", lb, 2)
    pass_on("r", rb, 0)
    relay("f", fb, 1, forward[1])
    relay("f", fb, 3, forward[3])
    pass_on("l", lb, 3)
    pass_on("r", rb, 1)
    arrived_all("l")
    pair(1, left)
    pass_on("f", fb, 0)
    pass_on("f", fb, 2)
    arrived_all("r")
    pair(2, right)
    pass_on("f", fb, 1)
    pass_on("f", fb, 3)
    first = pl.multiple_of(own * n_local, n_local)
    for c in icopies:
        c.wait_recv()
    routing_lists(jnp.concatenate([idx[b] for b in range(2 * n_x)], axis=1), first, n_local, lst_ref, cnt_ref)
    arrived_all("f")
    pair(3, far)
    n_hi = 2 * n_x * rows // LANES
    wl_ref[...] = jnp.zeros_like(wl_ref)
    for b in range(n_x):
        wt = prob[b, pl.ds(first, n_local), :]
        for e in range(n_local):
            for c in range(2):
                wl_ref[e * (n_hi + 1) + 2 * b + c:e * (n_hi + 1) + 2 * b + c + 1, :] = (
                    wt[e:e + 1, c * LANES:(c + 1) * LANES])
    for c in started + icopies:
        c.wait_send()
    for c in outs:
        c.wait()


def run_gather(hidden, idx_t, gain, rw_t, sig_t, shg_t, shu_t, n_local, n_x):
    rows, dim = hidden.shape
    n_tok = rows * 2 * n_x
    n_hi = n_tok // LANES
    n_exp, width = rw_t.shape[0], shg_t.shape[0]
    pad = (width + 15) // 16 * 16
    n_copy = 8 + 1 + 4 + 2 * 12 + 12
    n_peer = 2 * n_x - 1
    vmem = pl.BlockSpec(memory_space=pltpu.VMEM)
    hbm = pl.BlockSpec(memory_space=pl.ANY)
    return pl.pallas_call(
        functools.partial(gather_kernel, n_local),
        out_shape=(jax.ShapeDtypeStruct((n_tok, dim), BF16),
                   jax.ShapeDtypeStruct((width, n_tok), BF16),
                   jax.ShapeDtypeStruct((n_tok, 1), F32),
                   jax.ShapeDtypeStruct((n_local * n_hi, LANES), jnp.int32),
                   jax.ShapeDtypeStruct((n_local * (n_hi + 1), LANES), F32),
                   jax.ShapeDtypeStruct((n_local, LANES), jnp.int32)),
        in_specs=[hbm, hbm] + [vmem] * 5,
        out_specs=[hbm] + [vmem] * 5,
        scratch_shapes=[
            pltpu.VMEM((2 * n_x, rows, dim), BF16),
            pltpu.VMEM((2 * n_x,) + idx_t.shape, jnp.int32),
            pltpu.VMEM((n_exp + 2 * pad, dim), BF16),
            pltpu.VMEM((n_x, n_exp, 2 * rows), F32),
            pltpu.VMEM((n_x, 2 * rows, dim), BF16),
            pltpu.SemaphoreType.DMA((2,)),
            pltpu.SemaphoreType.DMA((n_copy,)),
            pltpu.SemaphoreType.DMA((n_copy,)),
            pltpu.SemaphoreType.DMA((n_peer,)),
            pltpu.SemaphoreType.DMA((n_peer,)),
            pltpu.SemaphoreType.DMA((n_x,)),
        ],
        compiler_params=pltpu.CompilerParams(collective_id=0, has_side_effects=True, vmem_limit_bytes=67_000_000),
        name="gather",
    )(hidden, idx_t, gain, rw_t, sig_t, shg_t, shu_t)


def expert_kernel(lst, wl, cnt, h_hbm, act_ref, sig_ref, shd_ref, wg_hbm, wu_hbm, wd_hbm, out_hbm,
                  h_in, table, acc, wg, wu, wd, xt, xb, fb, active, tile_e, tile_s, tile_r, tile_n,
                  in_sem, w_sem, out_sem):
    n_tok, dim = h_hbm.shape
    n_local = wg_hbm.shape[0]
    n_chunk = dim // LANES
    n_blocks = n_tok // LANES
    big = TILES[-1]
    stride = big + PAD

    def fetch_h(b):
        return pltpu.make_async_copy(h_hbm.at[pl.ds(b * LANES, LANES), :], h_in.at[b], in_sem.at[b])

    def weight_copies(e, s):
        return (pltpu.make_async_copy(wg_hbm.at[e], wg.at[s], w_sem.at[s, 0]),
                pltpu.make_async_copy(wu_hbm.at[e], wu.at[s], w_sem.at[s, 1]),
                pltpu.make_async_copy(wd_hbm.at[e], wd.at[s], w_sem.at[s, 2]))

    for b in range(n_blocks):
        fetch_h(b).start()

    def note(e, carry):
        n, tiles = carry
        total = cnt[e, 0]

        @pl.when(total > 0)
        def _():
            active[n] = e

        def tile(k, t):
            tile_e[t] = e
            tile_s[t] = n
            tile_r[t] = k * big
            tile_n[t] = jnp.minimum(total - k * big, big)
            return t + 1

        return n + jnp.where(total > 0, 1, 0), lax.fori_loop(0, (total + big - 1) // big, tile, tiles)

    n_active, n_tiles = lax.fori_loop(0, n_local, note, (0, 0))
    for s in range(SLOTS - 1):
        @pl.when(s < n_active)
        def _():
            for c in weight_copies(active[s], s):
                c.start()

    acc[n_tok * PITCH:, :] = jnp.zeros((acc.shape[0] - n_tok * PITCH, LANES), F32)
    table[n_tok * PITCH:, :] = jnp.zeros((table.shape[0] - n_tok * PITCH, LANES), F32)

    def shared(b, carry):
        rows = pl.ds(pl.multiple_of(b * LANES, LANES), LANES)
        sig = sig_ref[rows, :]
        for c in range(0, n_chunk, 2):
            sh = sig * lax.dot_general(act_ref[:, rows], shd_ref[:, c * LANES:(c + 2) * LANES], TN,
                                       preferred_element_type=F32)
            for d in range(2):
                acc[pl.ds(b * LANES * PITCH + c + d, LANES, stride=PITCH), :] = sh[:, d * LANES:(d + 1) * LANES]
        return carry

    lax.fori_loop(0, n_blocks, shared, 0)

    def spread(b, carry):
        fetch_h(b).wait()
        for c in range(n_chunk):
            table[pl.ds(b * LANES * PITCH + c, LANES, stride=PITCH), :] = (
                h_in[b, :, c * LANES:(c + 1) * LANES].astype(F32))
        return carry

    lax.fori_loop(0, n_blocks, spread, 0)

    def gather8(e, r0, g):
        base = e * n_tok + r0 + g * 8
        for i in range(8):
            t = lst[base + i]
            row = pl.multiple_of(t * PITCH, 4)
            xt[pl.ds(g * 8 + i, n_chunk, stride=stride), :] = table[pl.ds(row, n_chunk), :]

    def scatter8(e, r0, g):
        where, weight, old, new = [], [], [], []
        base = e * n_tok + r0 + g * 8
        for i in range(8):
            t = lst[base + i]
            where.append(pl.multiple_of(t * PITCH, 4))
            weight.append(wl[e * (n_tok + LANES) + t])
            old.append(acc[pl.ds(where[i], n_chunk), :])
        for i in range(8):
            new.append(old[i] + weight[i] * fb[pl.ds(g * 8 + i, n_chunk, stride=stride), :])
        for i in range(8):
            acc[pl.ds(where[i], n_chunk), :] = new[i]

    def ffn(m, s):
        for c in range(n_chunk):
            xb[:m, c * LANES:(c + 1) * LANES] = xt[c * stride:c * stride + m, :].astype(BF16)
        gate = lax.dot_general(wg[s], xb[:m, :], NT, preferred_element_type=F32)
        up = lax.dot_general(wu[s], xb[:m, :], NT, preferred_element_type=F32)
        act = (jax.nn.silu(gate) * up).astype(BF16)
        for c in range(0, n_chunk, 2):
            f = lax.dot_general(act, wd[s, :, c * LANES:(c + 2) * LANES], TN, preferred_element_type=F32)
            fb[c * stride:c * stride + m, :] = f[:, :LANES]
            fb[(c + 1) * stride:(c + 1) * stride + m, :] = f[:, LANES:]

    @pl.when(n_tiles > 0)
    def _():
        def first(g, carry):
            gather8(tile_e[0], tile_r[0], g)
            return carry

        lax.fori_loop(0, (tile_n[0] + 7) // 8, first, 0)

    def tile_step(i, carry):
        e, k, r0, n = tile_e[i], tile_s[i], tile_r[i], tile_n[i]
        s = lax.rem(k, SLOTS)

        @pl.when(r0 == 0)
        def _():
            ahead = k + SLOTS - 1

            @pl.when(ahead < n_active)
            def _():
                for c in weight_copies(active[ahead], lax.rem(ahead, SLOTS)):
                    c.start()

            for c in weight_copies(e, s):
                c.wait()

        below = 0
        for m in TILES:
            @pl.when((n > below) & (n <= m))
            def _(m=m):
                ffn(m, s)
            below = m

        last = i + 1 >= n_tiles
        nxt = jnp.where(last, i, i + 1)
        e2, r2 = tile_e[nxt], tile_r[nxt]
        n2 = jnp.where(last, 0, tile_n[nxt])
        both = (jnp.minimum(n, n2) + 7) // 8

        def mix(g, c2):
            gather8(e2, r2, g)
            scatter8(e, r0, g)
            return c2

        def more_in(g, c2):
            gather8(e2, r2, g)
            return c2

        def more_out(g, c2):
            scatter8(e, r0, g)
            return c2

        lax.fori_loop(0, both, mix, 0)
        lax.fori_loop(both, (n2 + 7) // 8, more_in, 0)
        lax.fori_loop(both, (n + 7) // 8, more_out, 0)
        return carry

    lax.fori_loop(0, n_tiles, tile_step, 0)

    def write_out(b):
        return pltpu.make_async_copy(h_in.at[b], out_hbm.at[pl.ds(b * LANES, LANES), :], out_sem.at[b])

    def finish(b, carry):
        for c in range(n_chunk):
            h_in[b, :, c * LANES:(c + 1) * LANES] = (
                acc[pl.ds(b * LANES * PITCH + c, LANES, stride=PITCH), :].astype(BF16))
        write_out(b).start()
        return carry

    lax.fori_loop(0, n_blocks, finish, 0)
    for b in range(n_blocks):
        write_out(b).wait()


def run_experts(lst, wl, cnt, h, act, sig, shd, wg, wu, wd):
    n_tok, dim = h.shape
    n_local, width, _ = wg.shape
    n_chunk = dim // LANES
    big = TILES[-1]
    max_tiles = n_local * ((n_tok + big - 1) // big)
    smem = pl.BlockSpec(memory_space=pltpu.SMEM)
    vmem = pl.BlockSpec(memory_space=pltpu.VMEM)
    hbm = pl.BlockSpec(memory_space=pl.ANY)
    return pl.pallas_call(
        expert_kernel,
        out_shape=jax.ShapeDtypeStruct((n_tok, dim), BF16),
        in_specs=[smem] * 3 + [hbm] + [vmem] * 3 + [hbm] * 3,
        out_specs=hbm,
        scratch_shapes=[
            pltpu.VMEM((n_tok // LANES, LANES, dim), BF16),
            pltpu.VMEM(((n_tok + 1) * PITCH, LANES), F32),
            pltpu.VMEM(((n_tok + 1) * PITCH, LANES), F32),
            pltpu.VMEM((SLOTS, width, dim), BF16),
            pltpu.VMEM((SLOTS, width, dim), BF16),
            pltpu.VMEM((SLOTS, width, dim), BF16),
            pltpu.VMEM((n_chunk * (big + PAD), LANES), F32),
            pltpu.VMEM((big, dim), BF16),
            pltpu.VMEM((n_chunk * (big + PAD), LANES), F32),
            pltpu.SMEM((n_local,), jnp.int32),
            pltpu.SMEM((max_tiles,), jnp.int32),
            pltpu.SMEM((max_tiles,), jnp.int32),
            pltpu.SMEM((max_tiles,), jnp.int32),
            pltpu.SMEM((max_tiles,), jnp.int32),
            pltpu.SemaphoreType.DMA((n_tok // LANES,)),
            pltpu.SemaphoreType.DMA((SLOTS, 3)),
            pltpu.SemaphoreType.DMA((n_tok // LANES,)),
        ],
        compiler_params=pltpu.CompilerParams(vmem_limit_bytes=67_000_000),
        name="experts",
    )(lst.reshape(-1), wl.reshape(-1), cnt, h, act, sig, shd, wg, wu, wd)


def reduce_kernel(groups, p_hbm, x_ref, out_ref, mate, own, ra, rb, rc, sems):
    x, core, y, n_x, n_y = place()
    rows, dim = x_ref.shape
    part = rows // n_y
    s_in, s_d, r_d, s_a, r_a, s_b, r_b, s_c, r_c, s_e, r_e = sems

    def at(v, n):
        return lax.rem(v + n, n)

    xs = [at(x + d, n_x) for d in range(4)]
    ys = [at(y + d, n_y) for d in range(4)]
    to_mate = peer(x, 1 - core, y)
    x_peers = [None] + [peer(xs[d], core, y) for d in range(1, 4)]
    y_peers = [None] + [peer(x, core, ys[d]) for d in range(1, 4)]
    mine = pl.ds(pl.multiple_of(y * part, part), part)
    started = []

    def go(c):
        c.start()
        started.append(c)
        return c

    loads, mates = [], []
    for g, (kind, lo, w) in enumerate(groups):
        c = pltpu.make_async_copy(p_hbm.at[:, core, :, lo:lo + w], own[g], s_in.at[g])
        c.start()
        loads.append(c)
    meet([to_mate] + x_peers[1:] + y_peers[1:])
    for g, (kind, lo, w) in enumerate(groups):
        mates.append(go(remote(p_hbm.at[:, 1 - core, :, lo:lo + w], mate[g], s_d.at[g], r_d.at[g], to_mate)))

    def unit(g, d, lo, n):
        if groups[g][0] == "x":
            return own[g].at[xs[d], lo:lo + n, :]
        return own[g].at[:, pl.ds(pl.multiple_of(ys[d] * part, part) + lo, n), :]

    def land(g, k, lo, n):
        return rb[g].at[k, lo:lo + n, :] if groups[g][0] == "x" else rb[g].at[k, :, lo:lo + n, :]

    def first_peers(g):
        return x_peers if groups[g][0] == "x" else y_peers

    def half(g):
        return (rows if groups[g][0] == "x" else part) // 2

    a, b_ind, b_dep, c_sent, e_sent = {}, {}, {}, {}, {}

    def add_mate(g):
        loads[g].wait()
        mates[g].wait_recv()
        own[g][...] = (own[g][...].astype(F32) + mate[g][...].astype(F32)).astype(BF16)
        h = half(g)
        for k, (lo, d) in enumerate(((0, 1), (h, 3))):
            a[g, k] = go(remote(unit(g, 2, lo, h), ra[g].at[k], s_a.at[g, k], r_a.at[g, k], first_peers(g)[d]))

    def send_near(g):
        h = half(g)
        for k, (lo, d) in enumerate(((h, 1), (0, 3))):
            b_ind[g, k] = go(remote(unit(g, d, lo, h), land(g, k, lo, h), s_b.at[g, k, 0], r_b.at[g, k, 0],
                                    first_peers(g)[d]))

    def add_far(g):
        h = half(g)
        for k, (lo, d) in enumerate(((0, 1), (h, 3))):
            a[g, k].wait_recv()
            ref = unit(g, d, lo, h)
            ref[...] = (ref[...].astype(F32) + ra[g][k].astype(F32)).astype(BF16)
            b_dep[g, k] = go(remote(ref, land(g, k, lo, h), s_b.at[g, k, 1], r_b.at[g, k, 1], first_peers(g)[d]))

    def second_axis(g):
        for k in range(2):
            b_ind[g, k].wait_recv()
            b_dep[g, k].wait_recv()
        ref = unit(g, 0, 0, 2 * half(g))
        ref[...] = (ref[...].astype(F32) + rb[g][0].astype(F32) + rb[g][1].astype(F32)).astype(BF16)
        for d in (2, 1, 3):
            if groups[g][0] == "x":
                src = own[g].at[x, pl.ds(pl.multiple_of(ys[d] * part, part), part), :]
                where = y_peers[d]
            else:
                src = own[g].at[xs[d], mine, :]
                where = x_peers[d]
            c_sent[g, d] = go(remote(src, rc[g].at[d - 1], s_c.at[g, d - 1], r_c.at[g, d - 1], where))

    def finish(g):
        kind, lo, w = groups[g]
        total = own[g][x, mine, :].astype(F32)
        for d in (1, 3, 2):
            c_sent[g, d].wait_recv()
            total = total + rc[g][d - 1].astype(F32)
        cols = slice(lo, lo + w)
        out_ref[mine, cols] = (x_ref[mine, cols].astype(F32) + total).astype(BF16)
        for d in (2, 1, 3):
            ref = out_ref.at[mine, cols]
            e_sent[g, d] = go(remote(ref, ref, s_e.at[g, d - 1], r_e.at[g, d - 1], y_peers[d]))

    order = ((add_mate, 0), (send_near, 0), (add_mate, 1), (send_near, 1), (add_mate, 2), (add_far, 0), (send_near, 2),
             (add_far, 1), (add_mate, 3), (add_far, 2), (second_axis, 1), (send_near, 3), (second_axis, 0),
             (add_mate, 4), (add_far, 3), (finish, 1), (send_near, 4), (second_axis, 2), (finish, 0), (add_far, 4),
             (second_axis, 3), (finish, 2), (second_axis, 4), (finish, 3), (finish, 4))
    for step, g in order:
        step(g)
    for g in range(len(groups)):
        for d in range(1, 4):
            e_sent[g, d].wait_recv()
    for c in started:
        c.wait_send()


def run_reduce(partial, hidden, n_x, n_y):
    rows, dim = hidden.shape
    q = dim // 8
    groups = (("x", 0, 2 * q), ("y", 2 * q, 2 * q), ("x", 4 * q, 2 * q), ("x", 6 * q, q), ("x", 7 * q, q))
    n_g = len(groups)
    part = rows // n_y
    dma = pltpu.SemaphoreType.DMA

    def per_group(of):
        return [pltpu.VMEM(of(kind, w), BF16) for kind, _, w in groups]

    def kernel(p, xr, o, *rest):
        lists = [rest[k * n_g:(k + 1) * n_g] for k in range(5)]
        reduce_kernel(groups, p, xr, o, *lists, rest[5 * n_g:])

    return pl.pallas_call(
        kernel,
        out_shape=jax.ShapeDtypeStruct((rows, dim), BF16),
        in_specs=[pl.BlockSpec(memory_space=pl.ANY), pl.BlockSpec(memory_space=pltpu.VMEM)],
        out_specs=pl.BlockSpec(memory_space=pltpu.VMEM),
        scratch_shapes=(
            per_group(lambda kind, w: (n_x, rows, w)) + per_group(lambda kind, w: (n_x, rows, w))
            + per_group(lambda kind, w: (2, rows // 2, w) if kind == "x" else (2, n_x, part // 2, w))
            + per_group(lambda kind, w: (2, rows, w) if kind == "x" else (2, n_x, part, w))
            + per_group(lambda kind, w: (3, part, w))
            + [dma((n_g,)), dma((n_g,)), dma((n_g,)), dma((n_g, 2)), dma((n_g, 2)), dma((n_g, 2, 2)),
               dma((n_g, 2, 2)), dma((n_g, 3)), dma((n_g, 3)), dma((n_g, 3)), dma((n_g, 3))]),
        compiler_params=pltpu.CompilerParams(collective_id=1, has_side_effects=True, vmem_limit_bytes=67_000_000),
        name="reduce",
    )(partial.reshape(n_x, 2, rows, dim), hidden)


def solution(mesh):
    tok_spec = P(('dp', 'ep'), None)
    in_specs = (tok_spec, tok_spec, P(None), P(None, None), P(None, None),
                P('ep', None, 'tp'), P('ep', None, 'tp'), P('ep', 'tp', None),
                P(None, ('tp', 'ep')), P(None, ('tp', 'ep')), P(('tp', 'ep'), None))
    n_x, n_y = mesh.shape['ep'] // 2, mesh.shape['tp']
    assert n_x == 4 and n_y == 4

    def local_step(hidden_in, topk_idx, norm_gain, router_w, shared_sig_w, exp_gate, exp_up, exp_down,
                   sh_gate, sh_up, sh_down):
        h, act, sig, lst, wl, cnt = run_gather(
            hidden_in, topk_idx.T, norm_gain.reshape(1, -1), router_w.T, shared_sig_w.T, sh_gate.T, sh_up.T,
            exp_gate.shape[0], n_x)
        partial = run_experts(lst, wl, cnt, h, act, sig, sh_down,
                              jnp.swapaxes(exp_gate, 1, 2), jnp.swapaxes(exp_up, 1, 2), exp_down)
        return run_reduce(partial, hidden_in, n_x, n_y)

    return jax.shard_map(local_step, mesh=mesh, in_specs=in_specs, out_specs=tok_spec, check_vma=False)
```

time: 96.2 us -> 90.9 us (0.945)
  the two profiles are of different devices: /device:TPU:97 before, /device:TPU:96 now
where the time goes in v4:
time: 90.9 us; the launch traced here: 89.9 us
  Pallas kernels  86.7 us (95%)
  local copies, waits for them, and re-layouts  3.17 us (3%)
    pallas_call x1, Pallas kernels, run_reduce(): pl.pallas_call(kernel, out_shape=jax.ShapeDtypeStruct((rows, dim), BF16),...  34.9 us
    pallas_call x1, Pallas kernels, run_gather(): pl.pallas_call(functools.partial(gather_kernel, n_local), out_shape=(jax....  27.2 us
    pallas_call x1, Pallas kernels, run_experts(): pl.pallas_call(expert_kernel, out_shape=jax.ShapeDtypeStruct((n_tok, dim)...  24.6 us
    unnamed x1, local copies, waits for them, and re-layouts  1.88 us

profile of v4, /device:TPU:96, one launch (start us, length us, event | category | flops | bytes accessed | tf_op | source)
XLA Modules:
  0.0 89.9 jit_solution(7717804404765664299)
XLA Ops:
  0.0 1.3 %reshape.12.gain_ref = bf16[1,2048]{1,0:T(2,128)(2,1)} reshape(bf16[2048]{0:T(1024)(128)(2,1)} %param.13) | data formatting | bytes 8192 | tf_op jit(solution)/shard_map/reshape | solution.py:645
  1.3 27.2 %gather.1 = (bf16[1024,2048]{1,0:T(8,128)(2,1)}, bf16[88,1024]{1,0:T(8,128)(2,1)}, f32[1024,1]{1,0:T(8,128)}, s32[64,128]{1,0:T(8,128)}, f32[72,128]{1,0:T(8,128)}, /*index=5*/s32[8,128]{1,0:T(8,128)}) custom-call(bf16[128,2048]{1,0:T(8,128)(2,1)} %xr.1, s32[6,128]{1,0:T(8,128)} %bitcast.19, bf16[1,2048]{1,0:T(2,128)(2,1)} %reshape.12.gain_ref, ...), custom_call_target="tpu_custom_call" | custom-call | tf_op jit(solution)/shard_map/gather/pallas_call | solution.py:255
  28.5 24.6 %experts.1 = bf16[1024,2048]{1,0:T(8,128)(2,1)} custom-call(s32[8192]{0:T(1024)} %bitcast.17, f32[9216]{0:T(1024)} %bitcast.16, s32[8,128]{1,0:T(8,128)} %get-tuple-element.13.cnt, bf16[1024,2048]{1,0:T(8,128)(2,1)} %get-tuple-element.14.h_hbm, bf16[88,1024]{1,0:T(8,128)(2,1)} %get-tuple-element.15.act_ref, f32[1024,1]{1,0:T(8,128)} %get-tuple-element.16.sig_ref, ...), custom_call_target="tpu_custom_call" | custom-call | tf_op jit(solution)/shard_map/experts/pallas_call | solution.py:464
  53.1 34.9 %reduce.1 = bf16[128,2048]{1,0:T(8,128)(2,1)} custom-call(bf16[4,2,128,2048]{3,2,1,0:T(8,128)(2,1)} %bitcast.10, bf16[128,2048]{1,0:T(8,128)(2,1)} %xr.1), custom_call_target="tpu_custom_call" | custom-call | tf_op jit(solution)/shard_map/reduce/pallas_call | solution.py:617
  88.0 1.9 %copy.13 = bf16[128,2048]{1,0:T(8,128)(2,1)} copy(bf16[128,2048]{1,0:T(8,128)(2,1)} %reduce.1) | data formatting | bytes 1048576
